TPU v7x, 64 devices: a 2x2x8 block of a 4x4x8 slice. The times are simulated.
64 devices in a mesh: rep: 4 (over x, y), dp: 16 (over z, core).
Axes of the slice: x: 2, y: 2, z: 8, core: 2. Of those that a mesh axis runs over, the one named last changes fastest.
The devices are a block of a 4x4x8 slice.
Arguments:
- g_w_gate: bfloat16 [64, 2, 512, 8192], P(('rep', 'dp')), parts along dimension 0
- g_w_up: bfloat16 [64, 2, 512, 8192], P(('rep', 'dp')), parts along dimension 0
- g_w_down: bfloat16 [64, 2, 8192, 512], P(('rep', 'dp')), parts along dimension 0
- w_gate: bfloat16 [2, 512, 8192], replicated
- w_up: bfloat16 [2, 512, 8192], replicated
- w_down: bfloat16 [2, 8192, 512], replicated
- m_w_gate: float32 [2, 512, 8192], P(None, 'dp')
- m_w_up: float32 [2, 512, 8192], P(None, 'dp')
- m_w_down: float32 [2, 8192, 512], P(None, 'dp')
- v_w_gate: float32 [2, 512, 8192], P(None, 'dp')
- v_w_up: float32 [2, 512, 8192], P(None, 'dp')
- v_w_down: float32 [2, 8192, 512], P(None, 'dp')
Outputs:
- output 1: bfloat16 [8, 512, 8192], P('rep'), parts along dimension 0
- output 2: bfloat16 [8, 512, 8192], P('rep'), parts along dimension 0
- output 3: bfloat16 [8, 8192, 512], P('rep'), parts along dimension 0
- output 4: float32 [8, 512, 8192], P('rep', 'dp'), parts along dimension 0
- output 5: float32 [8, 512, 8192], P('rep', 'dp'), parts along dimension 0
- output 6: float32 [8, 8192, 512], P('rep', 'dp'), parts along dimension 0
- output 7: float32 [8, 512, 8192], P('rep', 'dp'), parts along dimension 0
- output 8: float32 [8, 512, 8192], P('rep', 'dp'), parts along dimension 0
- output 9: float32 [8, 8192, 512], P('rep', 'dp'), parts along dimension 0
There are 4 independent parts. A program takes and returns all parts, laid end to end along the dimension named above; an argument that names none is the same for every part.
All inputs are finite; a program needn't handle non-finite values.
Results may differ from a plain program's by a relative error of at most 0.022.
Values are sent between devices in bfloat16 or wider.
A program may use at most 768 MiB of HBM per device.

v0:
```python
import jax
import jax.numpy as jnp
from jax import lax
from jax.sharding import PartitionSpec as P


def adamw(w, m, v, g):
    m = 0.9 * m + 0.1 * g
    v = 0.95 * v + 0.05 * g * g
    step = m * lax.rsqrt(v + 1e-8) + 0.1 * w
    return (w - 0.02 * step).astype(jnp.bfloat16), m, v


def clipped(gradients, sum_of_squares, count):
    factor = jnp.minimum(1.0, 0.5 * lax.rsqrt(sum_of_squares / count + 1e-30))
    return [g * factor for g in gradients]


def solution(mesh):
    def step(*arrays):
        terms, weights, m, v = (arrays[i : i + 3] for i in (0, 3, 6, 9))
        gradients = [lax.psum_scatter(t[0], "dp", scatter_dimension=1, tiled=True).astype(jnp.float32) for t in terms]
        squares = lax.psum(sum(jnp.sum(g * g) for g in gradients), "dp")
        gradients = clipped(gradients, squares, lax.psum(1, "dp") * sum(g.size for g in gradients))
        me = lax.axis_index("dp")
        own = [lax.dynamic_slice_in_dim(w, me * one.shape[1], one.shape[1], 1).astype(jnp.float32) for w, one in zip(weights, m, strict=True)]
        new = [adamw(w, m, v, g) for w, m, v, g in zip(own, m, v, gradients, strict=True)]
        whole = [lax.all_gather(one[0], "dp", axis=1, tiled=True) for one in new]
        return (*whole, *(one[1] for one in new), *(one[2] for one in new))

    all_of, cut = P(None, None, None), P(None, "dp", None)
    return jax.shard_map(
        step,
        mesh=mesh,
        in_specs=(P(("rep", "dp"), None, None, None),) * 3 + (all_of,) * 3 + (cut,) * 6,
        out_specs=(P("rep", None, None),) * 3 + (P("rep", "dp", None),) * 6,
        check_vma=False,
    )
```

profile of v0, /device:TPU:21, one launch (start us, length us, event | category | flops | bytes accessed | tf_op | source)
XLA Modules:
  0.0 662.2 jit_solution(5738523485628525838)
XLA Ops:
  7.3 0.7 reduce-scatter.4.cloned.1.call-update
  8.1 0.7 reduce-scatter.6.cloned.1.call-update
  8.9 0.7 reduce-scatter.8.cloned.1.call-update
  9.6 0.1 all-gather.8.cloned.1.call-start
  9.7 102.0 %reduce-scatter.4.cloned.1.call-done = bf16[2,32,8192]{2,1,0:T(8,128)(2,1)} async-done(((bf16[2,512,8192]{2,1,0:T(8,128)(2,1)}), bf16[2,32,8192]{2,1,0:T(8,128)(2,1)}) %reduce-scatter.4.cloned.1.call-update) | async-done | bytes 1048592 | tf_op jit(solution)/shard_map/reduce_scatter | solution.py:22
  111.7 2.4 fusion.9
  114.1 96.0 %reduce-scatter.6.cloned.1.call-done = bf16[2,32,8192]{2,1,0:T(8,128)(2,1)} async-done(((bf16[2,512,8192]{2,1,0:T(8,128)(2,1)}), bf16[2,32,8192]{2,1,0:T(8,128)(2,1)}) %reduce-scatter.6.cloned.1.call-update) | async-done | bytes 1048592 | tf_op jit(solution)/shard_map/reduce_scatter | solution.py:22
  210.1 2.4 fusion.10
  213.7 94.7 %reduce-scatter.8.cloned.1.call-done = bf16[2,512,512]{2,1,0:T(8,128)(2,1)} async-done(((bf16[2,8192,512]{2,1,0:T(8,128)(2,1)}), bf16[2,512,512]{2,1,0:T(8,128)(2,1)}) %reduce-scatter.8.cloned.1.call-update) | async-done | bytes 1048592 | tf_op jit(solution)/shard_map/reduce_scatter | solution.py:22
  308.4 2.4 fusion.11
  311.4 24.8 %psum.7 = f32[]{:T(128)} all-reduce(f32[]{:T(128)S(6)} %add.65), channel_id=1, replica_groups=mesh['rep'=4,'dp'=16] {'dp'}, use_global_device_ids=true, to_apply=%region_6.0 | all-reduce | flops 1 | bytes 8 | tf_op jit(solution)/shard_map/psum | solution.py:23
  336.9 5.3 fusion.17
  342.3 0.1 all-gather.4.cloned.1.call-start
  342.4 5.5 fusion.8
  348.0 0.1 all-gather.6.cloned.1.call-start
  348.1 5.5 fusion.14
  353.6 82.4 %all-gather.8.cloned.1.call-done = bf16[2,8192,512]{2,1,0:T(8,128)(2,1)} async-done(((bf16[2,512,512]{2,1,0:T(8,128)(2,1)}), bf16[2,8192,512]{2,1,0:T(8,128)(2,1)}) %all-gather.8.cloned.1.call-update) | async-done | bytes 16777232 | tf_op jit(solution)/shard_map/all_gather | solution.py:28
  436.0 92.6 %all-gather.4.cloned.1.call-done = bf16[2,512,8192]{2,1,0:T(8,128)(2,1)} async-done(((bf16[2,32,8192]{2,1,0:T(8,128)(2,1)}), bf16[2,512,8192]{2,1,0:T(8,128)(2,1)}) %all-gather.4.cloned.1.call-update) | async-done | bytes 16777232 | tf_op jit(solution)/shard_map/all_gather | solution.py:28
  528.6 92.6 %all-gather.6.cloned.1.call-done = bf16[2,512,8192]{2,1,0:T(8,128)(2,1)} async-done(((bf16[2,32,8192]{2,1,0:T(8,128)(2,1)}), bf16[2,512,8192]{2,1,0:T(8,128)(2,1)}) %all-gather.6.cloned.1.call-update) | async-done | bytes 16777232 | tf_op jit(solution)/shard_map/all_gather | solution.py:28
  621.3 16.7 %copy.24 = bf16[2,512,8192]{2,1,0:T(8,128)(2,1)} copy(bf16[2,512,8192]{2,1,0:T(8,128)(2,1)} %all-gather.4.cloned.1.call-done) | data formatting | bytes 33554432
  638.0 8.5 %copy.25 = bf16[2,512,8192]{2,1,0:T(8,128)(2,1)} copy(bf16[2,512,8192]{2,1,0:T(8,128)(2,1)S(1)} %copy-done) | data formatting | bytes 33554432
  646.5 1.3 slice-done.2
  647.8 1.4 slice-done.3
  649.2 6.2 copy.26
  (21 shorter events, 0.4 us)
Async XLA Ops:
  7.2 104.5 %reduce-scatter.4.cloned.1.call-start = ((), (), s32[]{:S(2)}) async-start(), calls=%async_computation.3 | async-start | bytes 17825792 | tf_op jit(solution)/shard_map/reduce_scatter | solution.py:22
  8.0 202.1 %reduce-scatter.6.cloned.1.call-start = ((), (), s32[]{:S(2)}) async-start(), calls=%async_computation.4 | async-start | bytes 17825792 | tf_op jit(solution)/shard_map/reduce_scatter | solution.py:22
  8.8 299.6 %reduce-scatter.8.cloned.1.call-start = ((), (), s32[]{:S(2)}) async-start(), calls=%async_computation.5 | async-start | bytes 17825792 | tf_op jit(solution)/shard_map/reduce_scatter | solution.py:22
  9.6 327.3 %copy-start.3 = (f32[2,512,512]{2,1,0:T(8,128)S(1)}, f32[2,512,512]{2,1,0:T(8,128)}, u32[]{:S(2)}) copy-start(f32[2,512,512]{2,1,0:T(8,128)} %param.23) | copy-start | bytes 6291460
  9.6 426.4 %all-gather.8.cloned.1.call-start = ((), (), s32[]{:S(2)}) async-start(), calls=%async_computation.8 | async-start | bytes 17825792 | tf_op jit(solution)/shard_map/all_gather | solution.py:28
  336.9 5.5 copy-start.2
  342.3 186.3 %all-gather.4.cloned.1.call-start = ((), (), s32[]{:S(2)}) async-start(), calls=%async_computation.6 | async-start | bytes 17825792 | tf_op jit(solution)/shard_map/all_gather | solution.py:28
  342.4 5.7 copy-start.1
  348.0 273.3 %all-gather.6.cloned.1.call-start = ((), (), s32[]{:S(2)}) async-start(), calls=%async_computation.7 | async-start | bytes 17825792 | tf_op jit(solution)/shard_map/all_gather | solution.py:28
  621.3 16.7 %copy-start = (bf16[2,512,8192]{2,1,0:T(8,128)(2,1)S(1)}, bf16[2,512,8192]{2,1,0:T(8,128)(2,1)}, u32[]{:S(2)}) copy-start(bf16[2,512,8192]{2,1,0:T(8,128)(2,1)} %all-gather.6.cloned.1.call-done) | copy-start | bytes 50331652
  621.3 25.2 %slice-start = ((s8[16777216]{0:T(1024)(128)(4,1)}), s8[4194304]{0:T(1024)(128)(4,1)S(1)}, s32[]{:S(2)}) async-start(s8[16777216]{0:T(1024)(128)(4,1)} %bitcast.6), calls=%async_computation.9 | async-start | bytes 8388608
  621.3 25.2 %slice-start.1 = ((s8[16777216]{0:T(1024)(128)(4,1)}), s8[4194304]{0:T(1024)(128)(4,1)S(1)}, s32[]{:S(2)}) async-start(s8[16777216]{0:T(1024)(128)(4,1)} %bitcast.6), calls=%async_computation.10 | async-start | bytes 8388608
  621.3 26.5 %slice-start.2 = ((s8[16777216]{0:T(1024)(128)(4,1)}), s8[4194304]{0:T(1024)(128)(4,1)S(1)}, s32[]{:S(2)}) async-start(s8[16777216]{0:T(1024)(128)(4,1)} %bitcast.6), calls=%async_computation.11 | async-start | bytes 8388608
  638.0 11.2 %slice-start.3 = ((s8[16777216]{0:T(1024)(128)(4,1)}), s8[4194304]{0:T(1024)(128)(4,1)S(1)}, s32[]{:S(2)}) async-start(s8[16777216]{0:T(1024)(128)(4,1)} %bitcast.6), calls=%async_computation.12 | async-start | bytes 8388608
Sparse Core Ops, SparseCore 0:
  10.4 101.3 reduce-scatter.3
  114.1 95.9 reduce-scatter.5
  212.4 95.9 reduce-scatter.7
  342.4 93.5 all-gather.7
  438.0 90.5 all-gather.3
  530.7 90.5 all-gather.5
where the time goes:
time: 662 us
  waiting for transfers between devices  563 us (85%)
  local copies, waits for them, and re-layouts  34.1 us (5%)
  blocking collectives  24.8 us (4%)
  other arithmetic  23.5 us (4%)
  between operations  16.9 us (3%)
    reduce_scatter x3, waiting for transfers between devices, step(): lax.psum_scatter(t[0], 'dp', scatter_dimension=1, tiled=True)  293 us
    all_gather x3, waiting for transfers between devices, step(): whole = [lax.all_gather(one[0], 'dp', axis=1, tiled=True) for one in new]  268 us
    unnamed x19, local copies, waits for them, and re-layouts  34.1 us
    psum x1, blocking collectives, step(): squares = lax.psum(sum((jnp.sum(g * g) for g in gradients)), 'dp')  24.8 us
    convert_element_type x3, other arithmetic, adamw(): return ((w - 0.02 * step).astype(jnp.bfloat16), m, v)  16.3 us
  transfers between devices with their start and end apart: 6, of which 6 were waited for; matrix products, arithmetic and copies ran while one was open for 2% of the time, Pallas kernels for 0%

commit v1 on v0

v1 whole, which is shorter than its diff:
```python
import functools

import jax
import jax.numpy as jnp
from jax import lax
from jax.experimental import pallas as pl
from jax.experimental.pallas import tpu as pltpu
from jax.sharding import PartitionSpec as P

MESH = pl.DeviceIdType.MESH
CORES = 2
PLUS, MINUS = 0, 1


def pieces_of(layers):
    return [(a, layer) for layer in range(layers) for a in range(3)]


def plan(n, layers):
    half = n // 2
    mine = lambda way: [q for q in pieces_of(layers) if (q[1] % 2 == 0) == (way == PLUS)]
    other = lambda way: [q for q in pieces_of(layers) if (q[1] % 2 == 0) != (way == PLUS)]
    queue = {}
    for way in (PLUS, MINUS):
        sends = [(way, half, q) for q in mine(way)]
        for d in range(half - 1, 0, -1):
            order = (other(way) + mine(way)) if d > 1 else (other(PLUS) + mine(PLUS))
            sends += [(way, d, q) for q in order]
        queue[way] = sends
    items = [s for pair in zip(queue[PLUS], queue[MINUS], strict=True) for s in pair]
    finals = [(None, 0, q) for q in other(PLUS) + mine(PLUS)]
    arrives = {}
    fresh = {}
    count = [0, 0]

    def slot(q):
        kind = int(q[0] == 2)
        count[kind] += 1
        return kind, count[kind] - 1

    for s in items:
        arrives[s] = slot(s[2])
    for s in items:
        way, d, q = s
        if (way, d + 1, q) not in arrives:
            fresh[s] = slot(q)
    return items, finals, arrives, fresh, count


def kernel(n, count_all, *refs):
    (gg, gu, gd, wg, wu, wd, mg, mu, md, vg, vu, vd) = refs[:12]
    (tg, tu, td, omg, omu, omd, ovg, ovu, ovd, xw, xd) = refs[12:23]
    (rw, rd, ow, od, pw, pd, mvw, mvd, bw, bd, ww, wwd, squares) = refs[23:36]
    (rs_send, rs_recv, x_send, x_recv, st_sem, ag_send, ag_recv, y_send, y_recv, sq_send, sq_recv, in_sem, out_sem) = refs[36:]

    g, w, m, v = (gg, gu, gd), (wg, wu, wd), (mg, mu, md), (vg, vu, vd)
    t, om, ov = (tg, tu, td), (omg, omu, omd), (ovg, ovu, ovd)
    layers = m[0].shape[0]
    rows = [a.shape[1] for a in m]
    items, finals, arrives, fresh, _ = plan(n, layers)
    pieces = pieces_of(layers)
    todo = items + finals
    half = n // 2
    devices = n * CORES

    me = lax.axis_index("dp")
    z, c = me // CORES, me % CORES
    at = lambda chip, core: lax.rem(chip + n, n) * CORES + core
    partner = at(z, 1 - c)
    ahead = {PLUS: at(z + 1, c), MINUS: at(z - 1, c)}
    step = {PLUS: 1, MINUS: -1}

    def block(ref, q, owner):
        a, layer = q
        r = pl.ds(pl.multiple_of(owner * rows[a], rows[a]), rows[a])
        return ref[a].at[layer, r]

    def term(q, owner):
        a, layer = q
        r = pl.ds(pl.multiple_of(owner * rows[a], rows[a]), rows[a])
        return g[a].at[0, layer, r]

    def remote(src, dst, send, recv, to):
        return pltpu.make_async_remote_copy(src_ref=src, dst_ref=dst, send_sem=send, recv_sem=recv, device_id={"dp": to}, device_id_type=MESH)

    barrier = pltpu.get_barrier_semaphore()
    for j in range(1, devices):
        pl.semaphore_signal(barrier, inc=1, device_id={"dp": lax.rem(me + j, devices)}, device_id_type=MESH)
    pl.semaphore_wait(barrier, devices - 1)

    x_at = []
    seen = [0, 0]
    for _, _, q in todo:
        kind = int(q[0] == 2)
        x_at.append((kind, seen[kind]))
        seen[kind] += 1
    xs, st_own, st_other, landed = (xw, xd), (ow, od), (pw, pd), (rw, rd)
    depth = [ow.shape[0], od.shape[0]]

    def target(way, d):
        return z if way is None else z + step[way] * d

    def exchange(i):
        way, d, q = todo[i]
        kind, k = x_at[i]
        return remote(term(q, at(target(way, d), 1 - c)), xs[kind].at[k], x_send.at[i], x_recv.at[i], partner)

    def stage(i):
        way, d, q = todo[i]
        kind, k = x_at[i]
        s = k % depth[kind]
        sem = kind * depth[0] + s
        return (
            pltpu.make_async_copy(term(q, at(target(way, d), c)), st_own[kind].at[s], st_sem.at[0, sem]),
            pltpu.make_async_copy(xs[kind].at[k], st_other[kind].at[s], st_sem.at[1, sem]),
        )

    def stage_start(i):
        exchange(i).wait_recv()
        for copy in stage(i):
            copy.start()

    def slices(kind, shape, size):
        if kind:
            r = max(16, size // shape[1])
            return shape[0] // r, lambda j: (pl.ds(pl.multiple_of(j * r, r), r), slice(None))
        cols = max(128, size // shape[0])
        return shape[1] // cols, lambda j: (slice(None), pl.ds(pl.multiple_of(j * cols, cols), cols))

    def added(dst, terms, kind, total=None):
        cuts, cut = slices(kind, dst.shape, 16384)

        def one(j, acc):
            part = cut(j)
            s = terms[0][part].astype(jnp.float32)
            for r in terms[1:]:
                s = s + r[part].astype(jnp.float32)
            s = s.astype(dst.dtype)
            dst[part] = s
            if acc is None:
                return None
            s = s.astype(jnp.float32)
            s = s * s
            s = jnp.sum(s.reshape(s.shape[0] // 8, 8, s.shape[1]), axis=0)
            for k in range(s.shape[1] // 128):
                acc = acc + s[:, k * 128 : (k + 1) * 128]
            return acc

        return lax.fori_loop(0, cuts, one, total)

    def ring(s):
        way, d, q = s
        kind, k = fresh[s] if s in fresh else arrives[(way, d + 1, q)]
        to_kind, to = arrives[s]
        i = items.index(s)
        return remote(landed[kind].at[k], landed[to_kind].at[to], rs_send.at[i], rs_recv.at[i], ahead[way])

    window = 12
    for i in range(window):
        exchange(i).start()
    reach = 2
    for i in range(reach):
        stage_start(i)
    moments = [(m, mvw, mvd, 0), (v, mvw, mvd, 1)]

    def held(which, q):
        a, layer = q
        if a == 2:
            return mvd.at[which, layer]
        return mvw.at[which, a * layers + layer]

    def weight(q):
        a, layer = q
        return bd.at[layer] if a == 2 else bw.at[a * layers + layer]

    def fresh_weight(q):
        a, layer = q
        return wwd.at[layer] if a == 2 else ww.at[a * layers + layer]

    def load_state(e):
        q = pieces[e]
        a, layer = q
        return (
            pltpu.make_async_copy(m[a].at[layer], held(0, q), in_sem.at[0, e]),
            pltpu.make_async_copy(v[a].at[layer], held(1, q), in_sem.at[1, e]),
            pltpu.make_async_copy(block(w, q, me), weight(q), in_sem.at[2, e]),
        )

    total = jnp.zeros((8, 128), jnp.float32)
    for i, s in enumerate(todo):
        way, d, q = s
        kind, k = x_at[i]
        for copy in stage(i):
            copy.wait()
        terms = [st_own[kind].at[k % depth[kind]], st_other[kind].at[k % depth[kind]]]
        if way is not None:
            if s not in fresh:
                before = (way, d + 1, q)
                ring(before).wait_recv()
                ak, ai = arrives[before]
                terms.append(landed[ak].at[ai])
                dst = landed[ak].at[ai]
            else:
                fk, fi = fresh[s]
                dst = landed[fk].at[fi]
            added(dst, terms, kind)
            ring(s).start()
        else:
            for w_ in (PLUS, MINUS):
                ring((w_, 1, q)).wait_recv()
                ak, ai = arrives[(w_, 1, q)]
                terms.append(landed[ak].at[ai])
            total = added(fresh_weight(q), terms, kind, total)
        if i + window < len(todo):
            exchange(i + window).start()
        if i + reach < len(todo):
            stage_start(i + reach)
        if 8 <= i < 8 + len(pieces):
            for copy in load_state(i - 8):
                copy.start()

    squares[me] = total

    def share(j, sender):
        to = lax.rem(me + j, devices)
        return remote(squares.at[sender], squares.at[sender], sq_send.at[j - 1], sq_recv.at[j - 1], to)

    for j in range(1, devices):
        share(j, me).start()
    for i in range(len(todo)):
        exchange(i).wait_send()
    for s in items:
        ring(s).wait_send()
    for e in range(len(pieces)):
        for copy in load_state(e):
            copy.wait()
    for j in range(1, devices):
        share(j, lax.rem(me - j + devices, devices)).wait_recv()
    everyone = jnp.sum(jnp.sum(squares[...], axis=0), axis=(0, 1), keepdims=True)
    factor = jnp.minimum(1.0, 0.5 * lax.rsqrt(jnp.broadcast_to(everyone, (8, 128)) / count_all + 1e-30))[0:1, 0:1]

    def stepped(q):
        kind = int(q[0] == 2)
        wn, mr, vr, wr = fresh_weight(q), held(0, q), held(1, q), weight(q)
        cuts, cut = slices(kind, wn.shape, 8192)

        def one(j, _):
            part = cut(j)
            grad = wn[part].astype(jnp.float32) * factor
            mm = 0.9 * mr[part] + 0.1 * grad
            vv = 0.95 * vr[part] + 0.05 * grad * grad
            mr[part] = mm
            vr[part] = vv
            old = wr[part].astype(jnp.float32)
            wn[part] = (old - 0.02 * (mm * lax.rsqrt(vv + 1e-8) + 0.1 * old)).astype(wn.dtype)
            return None

        lax.fori_loop(0, cuts, one, None)

    order = other_first = [q for q in pieces if q[1] % 2] + [q for q in pieces if not q[1] % 2]
    hops = {way: [(way, h, q) for h in range(1, half) for q in order] for way in (PLUS, MINUS)}
    for way in (PLUS, MINUS):
        hops[way] += [(way, half, q) for q in order if (q[1] % 2 == 1) == (way == PLUS)]
    gathers = [s for pair in zip(hops[PLUS], hops[MINUS], strict=True) for s in pair]

    def pass_on(s, arriving):
        way, h, q = s
        owner = at(z - step[way] * (h if arriving else h - 1), c)
        i = gathers.index(s)
        src = fresh_weight(q) if h == 1 and not arriving else block(t, q, owner)
        return remote(src, block(t, q, owner), ag_send.at[i], ag_recv.at[i], ahead[way])

    def across(i, arriving):
        core = 1 - c if arriving else c
        if i < len(gathers):
            way, h, q = gathers[i]
            owner = at(z - step[way] * h, core)
            src = block(t, q, owner)
        else:
            q = order[i - len(gathers)]
            owner = at(z, core)
            src = block(t, q, owner) if arriving else fresh_weight(q)
        return remote(src, block(t, q, owner), y_send.at[i], y_recv.at[i], partner)

    def results(e):
        q = pieces[e]
        a, layer = q
        return (
            pltpu.make_async_copy(held(0, q), om[a].at[layer], out_sem.at[0, e]),
            pltpu.make_async_copy(held(1, q), ov[a].at[layer], out_sem.at[1, e]),
            pltpu.make_async_copy(fresh_weight(q), block(t, q, me), out_sem.at[2, e]),
        )

    for q in order:
        stepped(q)
        for way in (PLUS, MINUS):
            pass_on((way, 1, q), False).start()
        across(len(gathers) + order.index(q), False).start()
        for copy in results(pieces.index(q)):
            copy.start()
    for i, s in enumerate(gathers):
        way, h, q = s
        pass_on(s, True).wait_recv()
        if (way, h + 1, q) in gathers:
            pass_on((way, h + 1, q), False).start()
        across(i, False).start()
    for j in range(1, devices):
        share(j, me).wait_send()
    for e in range(len(pieces)):
        for copy in results(e):
            copy.wait()
    for s in gathers:
        pass_on(s, False).wait_send()
    for i in range(len(gathers) + len(order)):
        across(i, False).wait_send()
    for i in range(len(gathers) + len(order)):
        across(i, True).wait_recv()


def solution(mesh):
    devices = mesh.shape["dp"]
    n = devices // CORES

    def step(*arrays):
        terms, weights, m, v = (arrays[i : i + 3] for i in (0, 3, 6, 9))
        layers = m[0].shape[0]
        items, finals, _, _, count = plan(n, layers)
        todo = items + finals
        wide, down = m[0].shape[1:], m[2].shape[1:]
        n_down = sum(q[0] == 2 for _, _, q in todo)
        hbm = pl.BlockSpec(memory_space=pl.ANY)
        bf, f32 = jnp.bfloat16, jnp.float32
        dma = pltpu.SemaphoreType.DMA
        sizes = devices * sum(one.size for one in m)
        pieces = len(pieces_of(layers))
        out = pl.pallas_call(
            functools.partial(kernel, n, sizes),
            out_shape=[jax.ShapeDtypeStruct(w.shape, bf) for w in weights]
            + [jax.ShapeDtypeStruct(one.shape, f32) for one in (*m, *v)]
            + [jax.ShapeDtypeStruct((len(todo) - n_down, *wide), bf), jax.ShapeDtypeStruct((n_down, *down), bf)],
            in_specs=[hbm] * 12,
            out_specs=[hbm] * 11,
            scratch_shapes=[
                pltpu.VMEM((count[0], *wide), bf),
                pltpu.VMEM((count[1], *down), bf),
                pltpu.VMEM((4, *wide), bf),
                pltpu.VMEM((2, *down), bf),
                pltpu.VMEM((4, *wide), bf),
                pltpu.VMEM((2, *down), bf),
                pltpu.VMEM((2, 2 * layers, *wide), f32),
                pltpu.VMEM((2, layers, *down), f32),
                pltpu.VMEM((2 * layers, *wide), bf),
                pltpu.VMEM((layers, *down), bf),
                pltpu.VMEM((2 * layers, *wide), bf),
                pltpu.VMEM((layers, *down), bf),
                pltpu.VMEM((devices, 8, 128), f32),
                dma((len(items),)),
                dma((len(items),)),
                dma((len(todo),)),
                dma((len(todo),)),
                dma((2, 6)),
                dma((len(items),)),
                dma((len(items),)),
                dma((len(todo),)),
                dma((len(todo),)),
                dma((devices - 1,)),
                dma((devices - 1,)),
                dma((3, pieces)),
                dma((3, pieces)),
            ],
            compiler_params=pltpu.CompilerParams(collective_id=0, has_side_effects=True, vmem_limit_bytes=60 * 2**20),
        )(*(t for t in terms), *weights, *m, *v)
        return tuple(out[:9])

    all_of, cut = P(None, None, None), P(None, "dp", None)
    return jax.shard_map(
        step,
        mesh=mesh,
        in_specs=(P(("rep", "dp"), None, None, None),) * 3 + (all_of,) * 3 + (cut,) * 6,
        out_specs=(P("rep", None, None),) * 3 + (P("rep", "dp", None),) * 6,
        check_vma=False,
    )
```

time: 662 us -> 552 us (0.83)
  waiting for transfers between devices: 563 us -> 0 us
  Pallas kernels: 0 us -> 503 us
  blocking collectives: 24.8 us -> 0 us
  other arithmetic: 23.5 us -> 0.01 us
  between operations: 16.9 us -> 0.7 us
  local copies, waits for them, and re-layouts: 34.1 us -> 47.2 us
    pallas_call x0 -> x1, Pallas kernels: none -> 503 us  [step(): pl.pallas_call(functools.partial(kernel, n, sizes), out_shape=[jax.ShapeD...]
    reduce_scatter x3 -> x0, waiting for transfers between devices: 293 us -> none  [step(): lax.psum_scatter(t[0], 'dp', scatter_dimension=1, tiled=True)]
    all_gather x3 -> x0, waiting for transfers between devices: 268 us -> none  [step(): whole = [lax.all_gather(one[0], 'dp', axis=1, tiled=True) for one in new]]
    psum x1 -> x0, blocking collectives: 24.8 us -> none  [step(): squares = lax.psum(sum((jnp.sum(g * g) for g in gradients)), 'dp')]
    convert_element_type x3 -> x0, other arithmetic: 16.3 us -> none  [adamw(): return ((w - 0.02 * step).astype(jnp.bfloat16), m, v)]
    unnamed x19 -> x31, local copies, waits for them, and re-layouts: 34.1 us -> 47.2 us
    reduce_sum x3 -> x0, other arithmetic: 7.11 us -> none  [step(): squares = lax.psum(sum((jnp.sum(g * g) for g in gradients)), 'dp')]
  transfers between devices with their start and end apart: 6 -> 0, of which waited for: 6 -> 0; matrix products, arithmetic and copies ran while one was open for 2% -> 0% of each run, Pallas kernels for 0% -> 0%
where the time goes in v1:
time: 552 us; the launch traced here: 551 us
  Pallas kernels  503 us (91%)
  local copies, waits for them, and re-layouts  47.2 us (9%)
    pallas_call x1, Pallas kernels, step(): pl.pallas_call(functools.partial(kernel, n, sizes), out_shape=[jax.ShapeD...  503 us
    unnamed x31, local copies, waits for them, and re-layouts  47.2 us

profile of v1, /device:TPU:21, one launch (start us, length us, event | category | flops | bytes accessed | tf_op | source)
XLA Modules:
  0.0 550.8 jit_solution(5796437899097211122)
XLA Ops:
  0.6 502.9 %shard_map.187 = (bf16[2,512,8192]{2,1,0:T(8,128)(2,1)}, bf16[2,512,8192]{2,1,0:T(8,128)(2,1)}, bf16[2,8192,512]{2,1,0:T(8,128)(2,1)}, f32[2,32,8192]{2,1,0:T(8,...) custom-call(bf16[1,2,512,8192]{3,2,1,0:T(8,128)(2,1)} %refs_0_.1, ...), custom_call_target="tpu_custom_call" | custom-call | tf_op jit(solution)/shard_map/pallas_call | solution.py:336
  503.5 0.0 copy-start
  503.5 0.0 slice-start
  503.5 0.0 slice-start.1
  503.5 16.7 %copy.30 = bf16[2,512,8192]{2,1,0:T(8,128)(2,1)} copy(bf16[2,512,8192]{2,1,0:T(8,128)(2,1)} %get-tuple-element.36) | data formatting | bytes 33554432
  520.2 0.0 copy-done
  520.2 8.5 %copy.31 = bf16[2,512,8192]{2,1,0:T(8,128)(2,1)} copy(bf16[2,512,8192]{2,1,0:T(8,128)(2,1)S(1)} %copy-done) | data formatting | bytes 33554432
  528.7 0.0 slice-done
  528.7 0.0 slice-done.1
  528.7 1.5 slice-done.2
  530.2 1.2 slice-done.3
  531.4 6.3 %copy.32 = bf16[2,8192,512]{2,1,0:T(8,128)(2,1)} copy(bf16[2,8192,512]{2,1,0:T(8,128)(2,1)S(1)} %bitcast.1) | data formatting | bytes 33554432
  537.7 0.0 copy-done.6
  537.7 1.3 copy.33
  539.0 1.0 copy-done.5
  540.1 1.3 copy.34
  541.4 1.0 copy-done.4
  542.4 1.3 copy.35
  543.7 1.0 copy-done.3
  544.8 1.3 copy.36
  546.1 1.0 copy-done.2
  547.1 1.3 copy.37
  548.4 1.0 copy-done.1
  549.5 1.3 copy.38
  (9 shorter events, 0.0 us)
Async XLA Ops:
  503.5 16.7 %copy-start = (bf16[2,512,8192]{2,1,0:T(8,128)(2,1)S(1)}, bf16[2,512,8192]{2,1,0:T(8,128)(2,1)}, u32[]{:S(2)}) copy-start(bf16[2,512,8192]{2,1,0:T(8,128)(2,1)} %get-tuple-element.37) | copy-start | bytes 50331652
  503.5 25.2 %slice-start = ((s8[16777216]{0:T(1024)(128)(4,1)}), s8[4194304]{0:T(1024)(128)(4,1)S(1)}, s32[]{:S(2)}) async-start(s8[16777216]{0:T(1024)(128)(4,1)} %bitcast), calls=%async_computation | async-start | bytes 8388608
  503.5 25.2 %slice-start.1 = ((s8[16777216]{0:T(1024)(128)(4,1)}), s8[4194304]{0:T(1024)(128)(4,1)S(1)}, s32[]{:S(2)}) async-start(s8[16777216]{0:T(1024)(128)(4,1)} %bitcast), calls=%async_computation.1 | async-start | bytes 8388608
  520.2 10.0 %slice-start.2 = ((s8[16777216]{0:T(1024)(128)(4,1)}), s8[4194304]{0:T(1024)(128)(4,1)S(1)}, s32[]{:S(2)}) async-start(s8[16777216]{0:T(1024)(128)(4,1)} %bitcast), calls=%async_computation.2 | async-start | bytes 8388608
  520.2 11.2 %slice-start.3 = ((s8[16777216]{0:T(1024)(128)(4,1)}), s8[4194304]{0:T(1024)(128)(4,1)S(1)}, s32[]{:S(2)}) async-start(s8[16777216]{0:T(1024)(128)(4,1)} %bitcast), calls=%async_computation.3 | async-start | bytes 8388608
  531.4 6.3 %copy-start.6 = (f32[2,32,8192]{2,1,0:T(8,128)S(1)}, f32[2,32,8192]{2,1,0:T(8,128)}, u32[]{:S(2)}) copy-start(f32[2,32,8192]{2,1,0:T(8,128)} %get-tuple-element.39) | copy-start | bytes 6291460
  537.7 2.3 copy-start.5
  540.1 2.3 copy-start.4
  542.4 2.3 copy-start.3
  544.8 2.3 copy-start.2
  547.1 2.3 copy-start.1

commit v2 on v1

--- a/solution.py
+++ b/solution.py
@@ -6,6 +6,7 @@
 from jax.experimental import pallas as pl
 from jax.experimental.pallas import tpu as pltpu
 from jax.sharding import PartitionSpec as P
+
 
 MESH = pl.DeviceIdType.MESH
 CORES = 2
@@ -47,11 +48,22 @@
     return items, finals, arrives, fresh, count
 
 
+def last_hop(way, layers):
+    return [q for q in pieces_of(layers) if (q[1] % 2 == 1) == (way == PLUS)]
+
+
+def last_slot(way, layers, q):
+    kind = int(q[0] == 2)
+    return kind, [p for p in last_hop(way, layers) if int(p[0] == 2) == kind].index(q)
+
+
 def kernel(n, count_all, *refs):
     (gg, gu, gd, wg, wu, wd, mg, mu, md, vg, vu, vd) = refs[:12]
     (tg, tu, td, omg, omu, omd, ovg, ovu, ovd, xw, xd) = refs[12:23]
-    (rw, rd, ow, od, pw, pd, mvw, mvd, bw, bd, ww, wwd, squares) = refs[23:36]
-    (rs_send, rs_recv, x_send, x_recv, st_sem, ag_send, ag_recv, y_send, y_recv, sq_send, sq_recv, in_sem, out_sem) = refs[36:]
+    last = {PLUS: refs[23:25], MINUS: refs[25:27]}
+    refs = refs[27:]
+    (rw, rd, ow, od, pw, pd, mvw, mvd, bw, bd, ww, wwd, squares) = refs[:13]
+    (rs_send, rs_recv, x_send, x_recv, st_sem, ag_send, ag_recv, y_send, y_recv, sq_send, sq_recv, in_sem, out_sem) = refs[13:]
 
     g, w, m, v = (gg, gu, gd), (wg, wu, wd), (mg, mu, md), (vg, vu, vd)
     t, om, ov = (tg, tu, td), (omg, omu, omd), (ovg, ovu, ovd)
@@ -161,7 +173,6 @@
     reach = 2
     for i in range(reach):
         stage_start(i)
-    moments = [(m, mvw, mvd, 0), (v, mvw, mvd, 1)]
 
     def held(which, q):
         a, layer = q
@@ -257,25 +268,28 @@
 
         lax.fori_loop(0, cuts, one, None)
 
-    order = other_first = [q for q in pieces if q[1] % 2] + [q for q in pieces if not q[1] % 2]
-    hops = {way: [(way, h, q) for h in range(1, half) for q in order] for way in (PLUS, MINUS)}
-    for way in (PLUS, MINUS):
-        hops[way] += [(way, half, q) for q in order if (q[1] % 2 == 1) == (way == PLUS)]
-    gathers = [s for pair in zip(hops[PLUS], hops[MINUS], strict=True) for s in pair]
+    order = [q for q in pieces if q[1] % 2] + [q for q in pieces if not q[1] % 2]
+    gathers = [(way, h, q) for h in range(1, half) for q in order for way in (PLUS, MINUS)]
+
+    def lies(way, h, q, owner):
+        if h == half - 1 and q in last_hop(way, layers):
+            kind, k = last_slot(way, layers, q)
+            return last[way][kind].at[k]
+        return block(t, q, owner)
 
     def pass_on(s, arriving):
         way, h, q = s
         owner = at(z - step[way] * (h if arriving else h - 1), c)
         i = gathers.index(s)
         src = fresh_weight(q) if h == 1 and not arriving else block(t, q, owner)
-        return remote(src, block(t, q, owner), ag_send.at[i], ag_recv.at[i], ahead[way])
+        return remote(src, lies(way, h, q, owner), ag_send.at[i], ag_recv.at[i], ahead[way])
 
     def across(i, arriving):
         core = 1 - c if arriving else c
         if i < len(gathers):
             way, h, q = gathers[i]
             owner = at(z - step[way] * h, core)
-            src = block(t, q, owner)
+            src = lies(way, h, q, owner)
         else:
             q = order[i - len(gathers)]
             owner = at(z, core)
@@ -317,29 +331,100 @@
         across(i, True).wait_recv()
 
 
+def moved(jobs, sem):
+    ins = [pltpu.make_async_copy(a, b, sem.at[0, j]) for j, (a, b, _) in enumerate(jobs)]
+    outs = [pltpu.make_async_copy(b, c, sem.at[1, j]) for j, (_, b, c) in enumerate(jobs)]
+    for copy in ins:
+        copy.start()
+    for copy, then in zip(ins, outs, strict=True):
+        copy.wait()
+        then.start()
+    for copy in outs:
+        copy.wait()
+
+
+def row_block(ref, layer, rows, owner):
+    return ref.at[layer, pl.ds(pl.multiple_of(owner * rows, rows), rows)]
+
+
+def settle(n, layers, arrays, rows, *refs):
+    k = len(arrays)
+    t, moments, last = refs[:k], refs[k : k + 3], {PLUS: refs[k + 3], MINUS: refs[k + 4]}
+    outs, new = refs[k + 5 : 2 * k + 5], refs[2 * k + 5 : 2 * k + 8]
+    buf, wide, down, sem = refs[2 * k + 8 :]
+    half = n // 2
+    me = lax.axis_index("dp")
+    z, c = me // CORES, me % CORES
+    jobs = []
+    for off in range(n):
+        if off == half:
+            continue
+        for core in (0, 1):
+            owner = lax.rem(z + off, n) * CORES + (c if core == 0 else 1 - c)
+            for j, a in enumerate(arrays):
+                for layer in range(layers):
+                    src = row_block(t[j], layer, rows, owner)
+                    for way, far in ((PLUS, n - (half - 1)), (MINUS, half - 1)):
+                        if core == 0 and off == far and (a, layer) in last_hop(way, layers):
+                            src = last[way].at[last_slot(way, layers, (a, layer))[1]]
+                    jobs.append((src, buf.at[len(jobs)], row_block(outs[j], layer, rows, owner)))
+    for a in range(3):
+        for layer in range(layers):
+            via = down.at[layer] if a == 2 else wide.at[a * layers + layer]
+            jobs.append((moments[a].at[layer], via, new[a].at[layer]))
+    moved(jobs, sem)
+
+
+def complete(n, layers, arrays, rows, *refs):
+    k = len(arrays)
+    came = {(way, core): refs[k + 2 * core + way] for core in (0, 1) for way in (PLUS, MINUS)}
+    outs, sem = refs[k + 4 : 2 * k + 4], refs[2 * k + 4]
+    me = lax.axis_index("dp")
+    z, c = me // CORES, me % CORES
+    copies = []
+    for (way, core), ref in came.items():
+        owner = lax.rem(z + n // 2, n) * CORES + (c if core == 0 else 1 - c)
+        for a, layer in last_hop(way, layers):
+            if a in arrays:
+                src = ref.at[last_slot(way, layers, (a, layer))[1]]
+                copies.append(pltpu.make_async_copy(src, row_block(outs[arrays.index(a)], layer, rows, owner), sem.at[len(copies)]))
+    for copy in copies:
+        copy.start()
+    for copy in copies:
+        copy.wait()
+
+
 def solution(mesh):
     devices = mesh.shape["dp"]
     n = devices // CORES
-
-    def step(*arrays):
-        terms, weights, m, v = (arrays[i : i + 3] for i in (0, 3, 6, 9))
+    hbm = pl.BlockSpec(memory_space=pl.ANY)
+    bf, f32 = jnp.bfloat16, jnp.float32
+    dma = pltpu.SemaphoreType.DMA
+    like = lambda a: jax.ShapeDtypeStruct(a.shape, a.dtype)
+    limit = pltpu.CompilerParams(vmem_limit_bytes=60 * 2**20)
+
+    def summed(terms, weights, m, v):
         layers = m[0].shape[0]
         items, finals, _, _, count = plan(n, layers)
         todo = items + finals
         wide, down = m[0].shape[1:], m[2].shape[1:]
         n_down = sum(q[0] == 2 for _, _, q in todo)
-        hbm = pl.BlockSpec(memory_space=pl.ANY)
-        bf, f32 = jnp.bfloat16, jnp.float32
-        dma = pltpu.SemaphoreType.DMA
         sizes = devices * sum(one.size for one in m)
         pieces = len(pieces_of(layers))
-        out = pl.pallas_call(
+        gathers = 2 * (n // 2 - 1) * pieces
+        lasts = []
+        for way in (PLUS, MINUS):
+            qs = last_hop(way, layers)
+            lasts.append(jax.ShapeDtypeStruct((sum(q[0] < 2 for q in qs), *wide), bf))
+            lasts.append(jax.ShapeDtypeStruct((sum(q[0] == 2 for q in qs), *down), bf))
+        return pl.pallas_call(
             functools.partial(kernel, n, sizes),
-            out_shape=[jax.ShapeDtypeStruct(w.shape, bf) for w in weights]
-            + [jax.ShapeDtypeStruct(one.shape, f32) for one in (*m, *v)]
-            + [jax.ShapeDtypeStruct((len(todo) - n_down, *wide), bf), jax.ShapeDtypeStruct((n_down, *down), bf)],
+            out_shape=[like(w) for w in weights]
+            + [like(one) for one in (*m, *v)]
+            + [jax.ShapeDtypeStruct((len(todo) - n_down, *wide), bf), jax.ShapeDtypeStruct((n_down, *down), bf)]
+            + lasts,
             in_specs=[hbm] * 12,
-            out_specs=[hbm] * 11,
+            out_specs=[hbm] * 15,
             scratch_shapes=[
                 pltpu.VMEM((count[0], *wide), bf),
                 pltpu.VMEM((count[1], *down), bf),
@@ -359,18 +444,77 @@
                 dma((len(todo),)),
                 dma((len(todo),)),
                 dma((2, 6)),
-                dma((len(items),)),
-                dma((len(items),)),
-                dma((len(todo),)),
-                dma((len(todo),)),
+                dma((gathers,)),
+                dma((gathers,)),
+                dma((gathers + pieces,)),
+                dma((gathers + pieces,)),
                 dma((devices - 1,)),
                 dma((devices - 1,)),
                 dma((3, pieces)),
                 dma((3, pieces)),
             ],
             compiler_params=pltpu.CompilerParams(collective_id=0, has_side_effects=True, vmem_limit_bytes=60 * 2**20),
-        )(*(t for t in terms), *weights, *m, *v)
-        return tuple(out[:9])
+            name="summed",
+        )(*terms, *weights, *m, *v)
+
+    def settled(arrays, t, moments, last):
+        layers, rows = moments[0].shape[0], moments[arrays[0]].shape[1]
+        jobs = CORES * (n - 1) * len(arrays) * layers
+        moved_bytes = 2 * (jobs * rows * t[0].shape[2] * 2 + 4 * sum(one.size for one in moments))
+        return pl.pallas_call(
+            functools.partial(settle, n, layers, arrays, rows),
+            out_shape=[like(one) for one in (*t, *moments)],
+            in_specs=[hbm] * (len(t) + 5),
+            out_specs=[hbm] * (len(t) + 3),
+            scratch_shapes=[
+                pltpu.VMEM((jobs, rows, t[0].shape[2]), bf),
+                pltpu.VMEM((2 * layers, *moments[0].shape[1:]), f32),
+                pltpu.VMEM((layers, *moments[2].shape[1:]), f32),
+                dma((2, jobs + 3 * layers)),
+            ],
+            compiler_params=limit,
+            cost_estimate=pl.CostEstimate(flops=60 * moved_bytes, bytes_accessed=moved_bytes, transcendentals=0),
+            name="settle",
+        )(*t, *moments, *last)
+
+    def completed(arrays, rows, results, came):
+        layers = results[0].shape[0]
+        jobs = CORES * len(arrays) * layers
+        return pl.pallas_call(
+            functools.partial(complete, n, layers, arrays, rows),
+            out_shape=[like(one) for one in results],
+            in_specs=[hbm] * len(results) + [pl.BlockSpec(memory_space=pltpu.VMEM)] * 4,
+            out_specs=[hbm] * len(results),
+            scratch_shapes=[dma((jobs,))],
+            input_output_aliases={i: i for i in range(len(results))},
+            compiler_params=pltpu.CompilerParams(vmem_limit_bytes=16 * 2**20),
+            name="complete",
+        )(*results, *came)
+
+    def step(*arrays):
+        terms, weights, m, v = (arrays[i : i + 3] for i in (0, 3, 6, 9))
+        out = summed(terms, weights, m, v)
+        t, new_m, new_v, last = out[:3], out[3:6], out[6:9], out[11:]
+        onward = [(i, (i + CORES) % devices) for i in range(devices)]
+        back = [(b, a) for a, b in onward]
+        other = [(i, i + 1 - 2 * (i % CORES)) for i in range(devices)]
+
+        def hop(k):
+            return [lax.ppermute(last[k], "dp", onward), lax.ppermute(last[2 + k], "dp", back)]
+
+        def cross(came):
+            return [lax.ppermute(one, "dp", other) for one in came]
+
+        rows = [one.shape[1] for one in m]
+        wide = hop(0)
+        down = hop(1)
+        g, u, *m = settled((0, 1), t[:2], new_m, (last[0], last[2]))
+        d, *v = settled((2,), t[2:], new_v, (last[1], last[3]))
+        wide += cross(wide)
+        down += cross(down)
+        g, u = completed((0, 1), rows[0], (g, u), wide)
+        (d,) = completed((2,), rows[2], (d,), down)
+        return (g, u, d, *m, *v)
 
     all_of, cut = P(None, None, None), P(None, "dp", None)
     return jax.shard_map(

time: 552 us -> 555 us (level)
  local copies, waits for them, and re-layouts: 47.2 us -> 0 us
  waiting for transfers between devices: 0 us -> 30.1 us
  Pallas kernels: 503 us -> 515 us
  starting transfers between devices: 0 us -> 8.25 us
    unnamed x31 -> x0, local copies, waits for them, and re-layouts: 47.2 us -> none
    ppermute x0 -> x8, waiting for transfers between devices: none -> 30.1 us  [the longest x2 30.1 us: hop(): lax.ppermute(last[k], 'dp', onward)]
    pallas_call x1 -> x5, Pallas kernels: 503 us -> 515 us  [the longest x1 470 us: summed(): pl.pallas_call(functools.partial(kernel, n, sizes), out_shape=[like(w) fo...]
    ppermute x0 -> x8, starting transfers between devices: none -> 8.25 us  [the longest x2 4.71 us: hop(): lax.ppermute(last[2 + k], 'dp', back)]
  transfers between devices with their start and end apart: 0 -> 8, of which waited for: 0 -> 2; matrix products, arithmetic and copies ran while one was open for 0% -> 0% of each run, Pallas kernels for 0% -> 8%
where the time goes in v2:
time: 555 us; the launch traced here: 554 us
  Pallas kernels  515 us (93%)
  waiting for transfers between devices  30.1 us (5%)
  starting transfers between devices  8.25 us (1%)
    pallas_call x1, Pallas kernels, summed(): pl.pallas_call(functools.partial(kernel, n, sizes), out_shape=[like(w) fo...  470 us
    pallas_call x2, Pallas kernels, settled(): pl.pallas_call(functools.partial(settle, n, layers, arrays, rows), out_sh...  39.5 us
    ppermute x2, waiting for transfers between devices, hop(): lax.ppermute(last[k], 'dp', onward)  30.1 us
  transfers between devices with their start and end apart: 8, of which 2 were waited for; matrix products, arithmetic and copies ran while one was open for 0% of the time, Pallas kernels for 8%

profile of v2, /device:TPU:21, one launch (start us, length us, event | category | flops | bytes accessed | tf_op | source)
XLA Modules:
  0.0 554.2 jit_solution(9807308288677116090)
XLA Ops:
  0.6 469.6 %summed.1 = (bf16[2,512,8192]{2,1,0:T(8,128)(2,1)}, bf16[2,512,8192]{2,1,0:T(8,128)(2,1)}, bf16[2,8192,512]{2,1,0:T(8,128)(2,1)}, f32[2,32,8192]{2,1,0:T(8,128)}...) custom-call(bf16[1,2,512,8192]{3,2,1,0:T(8,128)(2,1)} %refs_0_.1, ...), custom_call_target="tpu_custom_call" | custom-call | tf_op jit(solution)/shard_map/summed/pallas_call | solution.py:420
  470.2 0.7 collective-permute-start
  471.0 2.0 collective-permute-start.1
  473.0 0.0 collective-permute-start.4
  473.0 2.7 collective-permute-start.5
  475.7 20.6 %collective-permute-done.refs_2_ = bf16[2,32,8192]{2,1,0:T(8,128)(2,1)S(1)} collective-permute-done((bf16[2,32,8192]{2,1,0:T(8,128)(2,1)}, bf16[2,32,8192]{2,1,0:T(8,128)(2,1)S(1)}, u32[]{:S(2)}, u32[]{:S(2)}) %collective-permute-start) | collective-permute-done | bytes 1048608 | tf_op jit(solution)/shard_map/ppermute | solution.py:503
  496.2 1.7 collective-permute-start.2
  498.0 0.0 collective-permute-done.1.refs_3_
  498.0 0.0 collective-permute-start.3
  498.0 9.5 %collective-permute-done.4.refs_1_ = bf16[1,512,512]{2,1,0:T(8,128)(2,1)S(1)} collective-permute-done((bf16[1,512,512]{2,1,0:T(8,128)(2,1)}, bf16[1,512,512]{2,1,0:T(8,128)(2,1)S(1)}, u32[]{:S(2)}, u32[]{:S(2)}) %collective-permute-start.4) | collective-permute-done | bytes 524320 | tf_op jit(solution)/shard_map/ppermute | solution.py:503
  507.5 1.1 collective-permute-start.6
  508.5 0.0 collective-permute-done.5.refs_2_
  508.6 0.0 collective-permute-start.7
  508.6 15.0 %settle.3 = (bf16[2,8192,512]{2,1,0:T(8,128)(2,1)}, f32[2,32,8192]{2,1,0:T(8,128)}, f32[2,32,8192]{2,1,0:T(8,128)}, f32[2,512,512]{2,1,0:T(8,128)}) custom-call(bf16[2,8192,512]{2,1,0:T(8,128)(2,1)} %get-tuple-element.44.refs_0_, f32[2,32,8192]{2,1,0:T(8,128)} %get-tuple-element.45.refs_1_, f32[2,32,8192]{2,1,0:T(8,128)} %get-tuple-element.46.refs_2_, ...), custom_call_target="tpu_custom_call" | custom-call | flops 2516582400 | bytes 41943040 | tf_op jit(solution)/shard_map/settle/pallas_call | solution.py:464
  523.5 24.6 %settle.2 = (bf16[2,512,8192]{2,1,0:T(8,128)(2,1)}, bf16[2,512,8192]{2,1,0:T(8,128)(2,1)}, f32[2,32,8192]{2,1,0:T(8,128)}, f32[2,32,8192]{2,1,0:T(8,128)}, f32[2,512,512]{2,1,0:T(8,128)}) custom-call(bf16[2,512,8192]{2,1,0:T(8,128)(2,1)} %get-tuple-element.33.refs_0_, bf16[2,512,8192]{2,1,0:T(8,128)(2,1)} %get-tuple-element.34.refs_1_, ...), custom_call_target="tpu_custom_call" | custom-call | flops 4278190080 | bytes 71303168 | tf_op jit(solution)/shard_map/settle/pallas_call | solution.py:464
  548.1 0.0 collective-permute-done.6.refs_3_
  548.1 0.0 collective-permute-done.7.refs_4_
  548.1 2.7 complete.3
  550.8 0.0 collective-permute-done.2.refs_4_
  550.8 0.0 collective-permute-done.3.refs_5_
  550.9 3.3 complete.2
Async XLA Ops:
  470.2 26.0 %collective-permute-start = (bf16[2,32,8192]{2,1,0:T(8,128)(2,1)}, bf16[2,32,8192]{2,1,0:T(8,128)(2,1)S(1)}, u32[]{:S(2)}, u32[]{:S(2)}) collective-permute-start(bf16[2,32,8192]{2,1,0:T(8,128)(2,1)} %get-tuple-element.38.refs_5_), channel_id=1, source_target_pairs={{0,2},{1,3},{2,4},{3,5},{4,6},{5,7},{6,8},{7,9},{8,10},{9,11},{10,... | collective-permute-start | bytes 3145736 | tf_op jit(solution)/shard_map/ppermute | solution.py:503
  471.0 27.0 %collective-permute-start.1 = (bf16[2,32,8192]{2,1,0:T(8,128)(2,1)}, bf16[2,32,8192]{2,1,0:T(8,128)(2,1)S(1)}, u32[]{:S(2)}, u32[]{:S(2)}) collective-permute-start(bf16[2,32,8192]{2,1,0:T(8,128)(2,1)} %get-tuple-element.39.refs_6_), channel_id=1, source_target_pairs={{2,0},{3,1},{4,2},{5,3},{6,4},{7,5},{8,6},{9,7},{10,8},{11,9},{12,... | collective-permute-start | bytes 3145736 | tf_op jit(solution)/shard_map/ppermute | solution.py:503
  473.0 34.5 %collective-permute-start.4 = (bf16[1,512,512]{2,1,0:T(8,128)(2,1)}, bf16[1,512,512]{2,1,0:T(8,128)(2,1)S(1)}, u32[]{:S(2)}, u32[]{:S(2)}) collective-permute-start(bf16[1,512,512]{2,1,0:T(8,128)(2,1)} %get-tuple-element.48.refs_4_), channel_id=1, source_target_pairs={{0,2},{1,3},{2,4},{3,5},{4,6},{5,7},{6,8},{7,9},{8,10},{9,11},{10,... | collective-permute-start | bytes 1572872 | tf_op jit(solution)/shard_map/ppermute | solution.py:503
  473.0 35.6 %collective-permute-start.5 = (bf16[1,512,512]{2,1,0:T(8,128)(2,1)}, bf16[1,512,512]{2,1,0:T(8,128)(2,1)}, u32[]{:S(2)}, u32[]{:S(2)}) collective-permute-start(bf16[1,512,512]{2,1,0:T(8,128)(2,1)} %get-tuple-element.49.refs_5_), channel_id=1, source_target_pairs={{2,0},{3,1},{4,2},{5,3},{6,4},{7,5},{8,6},{9,7},{10,8},{11,9},{12,... | collective-permute-start | bytes 1572872 | tf_op jit(solution)/shard_map/ppermute | solution.py:503
  496.2 54.6 %collective-permute-start.2 = (bf16[2,32,8192]{2,1,0:T(8,128)(2,1)S(1)}, bf16[2,32,8192]{2,1,0:T(8,128)(2,1)S(1)}, u32[]{:S(2)}, u32[]{:S(2)}) collective-permute-start(bf16[2,32,8192]{2,1,0:T(8,128)(2,1)S(1)} %collective-permute-done.refs_2_), channel_id=1, source_target_pairs={{0,1},{1,0},{2,3},{3,2},{4,5},{5,4},{6,7},{7,6},{8,9},{9,8},{10,11... | collective-permute-start | bytes 3145736 | tf_op jit(solution)/shard_map/ppermute | solution.py:506
  498.0 52.9 %collective-permute-start.3 = (bf16[2,32,8192]{2,1,0:T(8,128)(2,1)S(1)}, bf16[2,32,8192]{2,1,0:T(8,128)(2,1)}, u32[]{:S(2)}, u32[]{:S(2)}) collective-permute-start(bf16[2,32,8192]{2,1,0:T(8,128)(2,1)S(1)} %collective-permute-done.1.refs_3_), channel_id=1, source_target_pairs={{0,1},{1,0},{2,3},{3,2},{4,5},{5,4},{6,7},{7,6},{8,9},{9,8},{10,11... | collective-permute-start | bytes 3145736 | tf_op jit(solution)/shard_map/ppermute | solution.py:506
  507.5 40.6 %collective-permute-start.6 = (bf16[1,512,512]{2,1,0:T(8,128)(2,1)S(1)}, bf16[1,512,512]{2,1,0:T(8,128)(2,1)}, u32[]{:S(2)}, u32[]{:S(2)}) collective-permute-start(bf16[1,512,512]{2,1,0:T(8,128)(2,1)S(1)} %collective-permute-done.4.refs_1_), channel_id=1, source_target_pairs={{0,1},{1,0},{2,3},{3,2},{4,5},{5,4},{6,7},{7,6},{8,9},{9,8},{10,11... | collective-permute-start | bytes 1572872 | tf_op jit(solution)/shard_map/ppermute | solution.py:506
  508.6 39.6 %collective-permute-start.7 = (bf16[1,512,512]{2,1,0:T(8,128)(2,1)}, bf16[1,512,512]{2,1,0:T(8,128)(2,1)}, u32[]{:S(2)}, u32[]{:S(2)}) collective-permute-start(bf16[1,512,512]{2,1,0:T(8,128)(2,1)} %collective-permute-done.5.refs_2_), channel_id=1, source_target_pairs={{0,1},{1,0},{2,3},{3,2},{4,5},{5,4},{6,7},{7,6},{8,9},{9,8},{10,11... | collective-permute-start | bytes 1572872 | tf_op jit(solution)/shard_map/ppermute | solution.py:506

commit v3 on v1

v3 whole, which is shorter than its diff:
```python
import functools

import jax
import jax.numpy as jnp
from jax import lax
from jax.experimental import pallas as pl
from jax.experimental.pallas import tpu as pltpu
from jax.sharding import PartitionSpec as P


MESH = pl.DeviceIdType.MESH
CORES = 2
PLUS, MINUS = WAYS = 0, 1
PARTS = 2
DOWN = 2


def pieces_of(layers):
    return [(a, layer, part) for part in range(PARTS) for layer in range(layers) for a in range(3)]


def kind_of(q):
    return int(q[0] == DOWN)


def place(q, among):
    return kind_of(q), [p for p in among if kind_of(p) == kind_of(q)].index(q)


def counts(among):
    return [sum(kind_of(q) == kind for q in among) for kind in (0, 1)]


def half_of(way, layers):
    return [q for q in pieces_of(layers) if q[2] % 2 == way]


def far_half(way, layers):
    return half_of(1 - way, layers)


def plan(n, layers):
    half = n // 2
    queue = {}
    for way in WAYS:
        mine, other = half_of(way, layers), half_of(1 - way, layers)
        sends = [(way, half, q) for q in mine]
        for d in range(half - 1, 0, -1):
            sends += [(way, d, q) for q in (other + mine if d > 1 else pieces_of(layers))]
        queue[way] = sends
    items = [s for pair in zip(queue[PLUS], queue[MINUS], strict=True) for s in pair]
    finals = [(None, 0, q) for q in pieces_of(layers)]
    arrives = {}
    fresh = {}
    count = [0, 0]

    def slot(q):
        count[kind_of(q)] += 1
        return kind_of(q), count[kind_of(q)] - 1

    for s in items:
        arrives[s] = slot(s[2])
    for s in items:
        if (s[0], s[1] + 1, s[2]) not in arrives:
            fresh[s] = slot(s[2])
    return items, finals, arrives, fresh, count


def kernel(n, count_all, *refs):
    g, w, m, v, t = (refs[i : i + 3] for i in range(0, 15, 3))
    xs, ms, vs, own_new = (refs[i : i + 2] for i in range(15, 23, 2))
    far = {way: refs[23 + 2 * way : 25 + 2 * way] for way in WAYS}
    near = {way: refs[27 + 2 * way : 29 + 2 * way] for way in WAYS}
    landed, st_own, st_other, old = (refs[i : i + 2] for i in range(31, 39, 2))
    squares, rs_send, rs_recv, x_send, x_recv, st_sem, ag_send, ag_recv, y_send, y_recv, sq_send, sq_recv, in_sem, _ = refs[39:]

    layers = m[0].shape[0]
    rows = [a.shape[1] for a in m]
    items, finals, arrives, fresh, _ = plan(n, layers)
    pieces = pieces_of(layers)
    todo = items + finals
    half = n // 2
    devices = n * CORES

    me = lax.axis_index("dp")
    z, c = me // CORES, me % CORES
    at = lambda chip, core: lax.rem(chip + n, n) * CORES + core
    partner = at(z, 1 - c)
    ahead = {PLUS: at(z + 1, c), MINUS: at(z - 1, c)}
    step = {PLUS: 1, MINUS: -1}

    def rows_of(q, owner):
        size = rows[q[0]] // PARTS
        return pl.ds(pl.multiple_of(owner * rows[q[0]] + q[2] * size, size), size)

    def block(ref, q, owner):
        return ref[q[0]].at[q[1], rows_of(q, owner)]

    def term(q, owner):
        return g[q[0]].at[0, q[1], rows_of(q, owner)]

    def kept(pair, q):
        kind, k = place(q, pieces)
        return pair[kind].at[k]

    def remote(src, dst, send, recv, to):
        return pltpu.make_async_remote_copy(src_ref=src, dst_ref=dst, send_sem=send, recv_sem=recv, device_id={"dp": to}, device_id_type=MESH)

    barrier = pltpu.get_barrier_semaphore()
    for to in (partner, ahead[PLUS], ahead[MINUS]):
        pl.semaphore_signal(barrier, inc=1, device_id={"dp": to}, device_id_type=MESH)
    pl.semaphore_wait(barrier, 3)

    x_at = []
    for _, _, q in todo:
        x_at.append((kind_of(q), sum(kind == kind_of(q) for kind, _ in x_at)))
    depth = [ref.shape[0] for ref in st_own]

    def target(way, d):
        return z if way is None else z + step[way] * d

    def exchange(i):
        way, d, q = todo[i]
        kind, k = x_at[i]
        return remote(term(q, at(target(way, d), 1 - c)), xs[kind].at[k], x_send.at[i], x_recv.at[i], partner)

    def stage(i):
        way, d, q = todo[i]
        kind, k = x_at[i]
        s = k % depth[kind]
        sem = kind * depth[0] + s
        return (
            pltpu.make_async_copy(term(q, at(target(way, d), c)), st_own[kind].at[s], st_sem.at[0, sem]),
            pltpu.make_async_copy(xs[kind].at[k], st_other[kind].at[s], st_sem.at[1, sem]),
        )

    def stage_start(i):
        exchange(i).wait_recv()
        for copy in stage(i):
            copy.start()

    def slices(kind, shape, size):
        if kind:
            r = max(16, size // shape[1])
            return shape[0] // r, lambda j: (pl.ds(pl.multiple_of(j * r, r), r), slice(None))
        cols = max(128, size // shape[0])
        return shape[1] // cols, lambda j: (slice(None), pl.ds(pl.multiple_of(j * cols, cols), cols))

    def added(dst, terms, kind, total=None):
        cuts, cut = slices(kind, dst.shape, 16384)

        def one(j, acc):
            part = cut(j)
            s = terms[0][part].astype(jnp.float32)
            for r in terms[1:]:
                s = s + r[part].astype(jnp.float32)
            s = s.astype(dst.dtype)
            dst[part] = s
            if acc is None:
                return None
            s = s.astype(jnp.float32)
            s = s * s
            s = jnp.sum(s.reshape(s.shape[0] // 8, 8, s.shape[1]), axis=0)
            for k in range(s.shape[1] // 128):
                acc = acc + s[:, k * 128 : (k + 1) * 128]
            return acc

        return lax.fori_loop(0, cuts, one, total)

    def ring(s):
        way, d, q = s
        kind, k = fresh[s] if s in fresh else arrives[(way, d + 1, q)]
        to_kind, to = arrives[s]
        i = items.index(s)
        return remote(landed[kind].at[k], landed[to_kind].at[to], rs_send.at[i], rs_recv.at[i], ahead[way])

    def load_state(e):
        q = pieces[e]
        part = (q[1], pl.ds(q[2] * (rows[q[0]] // PARTS), rows[q[0]] // PARTS))
        return (
            pltpu.make_async_copy(m[q[0]].at[part], kept(ms, q), in_sem.at[0, e]),
            pltpu.make_async_copy(v[q[0]].at[part], kept(vs, q), in_sem.at[1, e]),
            pltpu.make_async_copy(block(w, q, me), kept(old, q), in_sem.at[2, e]),
        )

    window, reach = 24, 3
    for i in range(window):
        exchange(i).start()
    for i in range(reach):
        stage_start(i)
    total = jnp.zeros((8, 128), jnp.float32)
    for i, s in enumerate(todo):
        way, d, q = s
        kind, k = x_at[i]
        for copy in stage(i):
            copy.wait()
        terms = [st_own[kind].at[k % depth[kind]], st_other[kind].at[k % depth[kind]]]
        if way is not None:
            if s not in fresh:
                ring((way, d + 1, q)).wait_recv()
                kind, k = arrives[(way, d + 1, q)]
                terms.append(landed[kind].at[k])
            else:
                kind, k = fresh[s]
            added(landed[kind].at[k], terms, kind)
            ring(s).start()
        else:
            for from_ in WAYS:
                ring((from_, 1, q)).wait_recv()
                kind, k = arrives[(from_, 1, q)]
                terms.append(landed[kind].at[k])
            total = added(kept(own_new, q), terms, kind, total)
        if i + window < len(todo):
            exchange(i + window).start()
        if i + reach < len(todo):
            stage_start(i + reach)
        if 12 <= i < 12 + len(pieces):
            for copy in load_state(i - 12):
                copy.start()

    squares[me] = total

    def share(j, sender):
        to = lax.rem(me + j, devices)
        return remote(squares.at[sender], squares.at[sender], sq_send.at[j - 1], sq_recv.at[j - 1], to)

    for j in range(1, devices):
        share(j, me).start()
    for i in range(len(todo)):
        exchange(i).wait_send()
    for s in items:
        ring(s).wait_send()
    for e in range(len(pieces)):
        for copy in load_state(e):
            copy.wait()
    for j in range(1, devices):
        share(j, lax.rem(me - j + devices, devices)).wait_recv()
    everyone = jnp.sum(jnp.sum(squares[...], axis=0), axis=(0, 1), keepdims=True)
    factor = jnp.minimum(1.0, 0.5 * lax.rsqrt(jnp.broadcast_to(everyone, (8, 128)) / count_all + 1e-30))[0:1, 0:1]

    def stepped(q):
        wn, mr, vr, wr = kept(own_new, q), kept(ms, q), kept(vs, q), kept(old, q)
        cuts, cut = slices(kind_of(q), wn.shape, 8192)

        def one(j, _):
            part = cut(j)
            grad = wn[part].astype(jnp.float32) * factor
            mm = 0.9 * mr[part] + 0.1 * grad
            vv = 0.95 * vr[part] + 0.05 * grad * grad
            mr[part] = mm
            vr[part] = vv
            before = wr[part].astype(jnp.float32)
            wn[part] = (before - 0.02 * (mm * lax.rsqrt(vv + 1e-8) + 0.1 * before)).astype(wn.dtype)
            return None

        lax.fori_loop(0, cuts, one, None)

    gathers = [(way, h, q) for h in range(1, half) for q in pieces for way in WAYS]

    def lies(way, h, q, owner):
        if h < half - 1:
            return block(t, q, owner)
        which, among = (far, far_half(way, layers)) if q in far_half(way, layers) else (near, half_of(way, layers))
        kind, k = place(q, among)
        return which[way][kind].at[k]

    def pass_on(s, arriving):
        way, h, q = s
        owner = at(z - step[way] * (h if arriving else h - 1), c)
        i = gathers.index(s)
        src = kept(own_new, q) if h == 1 and not arriving else block(t, q, owner)
        return remote(src, lies(way, h, q, owner), ag_send.at[i], ag_recv.at[i], ahead[way])

    def across(i, arriving):
        core = 1 - c if arriving else c
        if i < len(gathers):
            way, h, q = gathers[i]
            owner = at(z - step[way] * h, core)
            src = lies(way, h, q, owner)
        else:
            q = pieces[i - len(gathers)]
            owner = at(z, core)
            src = kept(own_new, q)
        return remote(src, block(t, q, owner), y_send.at[i], y_recv.at[i], partner)

    for e, q in enumerate(pieces):
        stepped(q)
        for way in WAYS:
            pass_on((way, 1, q), False).start()
        across(len(gathers) + e, False).start()
    for i, s in enumerate(gathers):
        way, h, q = s
        pass_on(s, True).wait_recv()
        if h + 1 < half:
            pass_on((way, h + 1, q), False).start()
        across(i, False).start()
    for j in range(1, devices):
        share(j, me).wait_send()
    for s in gathers:
        pass_on(s, False).wait_send()
    for i in range(len(gathers) + len(pieces)):
        across(i, False).wait_send()
    for i in range(len(gathers) + len(pieces)):
        across(i, True).wait_recv()


def moved(jobs, sem):
    ins = [pltpu.make_async_copy(a, b, sem.at[0, j]) if b is not None else None for j, (a, b, _) in enumerate(jobs)]
    outs = [pltpu.make_async_copy(a if b is None else b, c, sem.at[1, j]) for j, (a, b, c) in enumerate(jobs)]
    for copy in ins:
        if copy is not None:
            copy.start()
    for copy, then in zip(ins, outs, strict=True):
        if copy is None:
            then.start()
    for copy, then in zip(ins, outs, strict=True):
        if copy is not None:
            copy.wait()
            then.start()
    for copy in outs:
        copy.wait()


def row_part(ref, layer, part, rows, owner):
    size = rows // PARTS
    return ref.at[layer, pl.ds(pl.multiple_of(owner * rows + part * size, size), size)]


def moment_jobs(pair, results, layers):
    pieces = pieces_of(layers)
    jobs = []
    for q in pieces:
        a, layer, part = q
        kind, k = place(q, pieces)
        size = results[a].shape[1] // PARTS
        jobs.append((pair[kind].at[k], None, results[a].at[layer, pl.ds(part * size, size)]))
    return jobs


def settle(n, layers, arrays, rows, moment, *refs):
    k = len(arrays)
    t, own, refs = refs[:k], refs[k], refs[k + 1 :]
    far, near, refs = refs[0:2], refs[2:4], refs[4:]
    pair, refs = (refs[:2], refs[2:]) if moment else (None, refs)
    outs, refs = refs[:k], refs[k:]
    results, refs = (refs[:3], refs[3:]) if moment else (None, refs)
    buf, sem = refs
    half = n // 2
    me = lax.axis_index("dp")
    z, c = me // CORES, me % CORES
    pieces = pieces_of(layers)
    jobs = moment_jobs(pair, results, layers) if moment else []
    through = 0
    for off in range(n):
        if off == half:
            continue
        for core in range(CORES):
            owner = lax.rem(z + off, n) * CORES + (c if core == 0 else 1 - c)
            for q in pieces:
                a, layer, part = q
                if a not in arrays:
                    continue
                dst = row_part(outs[arrays.index(a)], layer, part, rows, owner)
                src = None
                if core == 0 and off == 0:
                    src = own.at[place(q, pieces)[1]]
                for way, come in ((PLUS, n - (half - 1)), (MINUS, half - 1)):
                    if core == 0 and off == come:
                        which, among = (far, far_half(way, layers)) if q in far_half(way, layers) else (near, half_of(way, layers))
                        src = which[way].at[place(q, among)[1]]
                if src is not None:
                    jobs.append((src, None, dst))
                else:
                    jobs.append((row_part(t[arrays.index(a)], layer, part, rows, owner), buf.at[through], dst))
                    through += 1
    moved(jobs, sem)


def settle_moment(layers, *refs):
    moved(moment_jobs(refs[:2], refs[2:5], layers), refs[5])


def complete(n, layers, rows, *refs):
    came, outs, sem = refs[3:11], refs[11:14], refs[14]
    me = lax.axis_index("dp")
    z, c = me // CORES, me % CORES
    jobs = []
    for core in range(CORES):
        owner = lax.rem(z + n // 2, n) * CORES + (c if core == 0 else 1 - c)
        for way in WAYS:
            for q in far_half(way, layers):
                kind, k = place(q, far_half(way, layers))
                jobs.append((came[4 * kind + 2 * core + way].at[k], None, row_part(outs[q[0]], q[1], q[2], rows[q[0]], owner)))
    moved(jobs, sem)


def solution(mesh):
    devices = mesh.shape["dp"]
    n = devices // CORES
    hbm, vmem = pl.BlockSpec(memory_space=pltpu.HBM), pl.BlockSpec(memory_space=pltpu.VMEM)
    bf, f32 = jnp.bfloat16, jnp.float32
    dma = pltpu.SemaphoreType.DMA
    like = lambda a: jax.ShapeDtypeStruct(a.shape, a.dtype)

    def params(mib, **more):
        return pltpu.CompilerParams(vmem_limit_bytes=mib * 2**20, **more)

    def summed(terms, weights, m, v):
        layers = m[0].shape[0]
        items, finals, _, _, count = plan(n, layers)
        pieces = pieces_of(layers)
        todo = items + finals
        shapes = [(m[a].shape[1] // PARTS, m[a].shape[2]) for a in (0, DOWN)]
        pair = lambda make, number, dtype: [make((number[kind], *shapes[kind]), dtype) for kind in (0, 1)]
        whole, part = counts(pieces), counts(half_of(PLUS, layers))
        hops = 2 * (n // 2 - 1) * len(pieces)
        outs = [like(w) for w in weights] + pair(jax.ShapeDtypeStruct, counts([s[2] for s in todo]), bf)
        held = 2 * pair(pltpu.VMEM, whole, f32) + pair(pltpu.VMEM, whole, bf) + 4 * pair(pltpu.VMEM, part, bf)
        return pl.pallas_call(
            functools.partial(kernel, n, devices * sum(one.size for one in m)),
            out_shape=outs + held,
            in_specs=[hbm] * 12,
            out_specs=[hbm] * len(outs) + [vmem] * len(held),
            scratch_shapes=pair(pltpu.VMEM, count, bf)
            + 2 * pair(pltpu.VMEM, (4, 2), bf)
            + pair(pltpu.VMEM, whole, bf)
            + [pltpu.VMEM((devices, 8, 128), f32)]
            + [dma((len(items),))] * 2
            + [dma((len(todo),))] * 2
            + [dma((2, 6))]
            + [dma((hops,))] * 2
            + [dma((hops + len(pieces),))] * 2
            + [dma((devices - 1,))] * 2
            + [dma((3, len(pieces)))] * 2,
            compiler_params=params(38, collective_id=0, has_side_effects=True),
            name="summed",
        )(*terms, *weights, *m, *v)

    def settled(arrays, t, own, far, near, m, moment=()):
        layers, rows = m[0].shape[0], m[arrays[0]].shape[1]
        through = ((n - 1) * CORES - 3) * len(arrays) * layers * PARTS
        jobs = (n - 1) * CORES * len(arrays) * layers * PARTS + (len(pieces_of(layers)) if moment else 0)
        size = rows // PARTS * t[0].shape[2]
        moved_bytes = 2 * size * (jobs + through)
        results = [like(one) for one in m] if moment else []
        return pl.pallas_call(
            functools.partial(settle, n, layers, arrays, rows, bool(moment)),
            out_shape=[like(one) for one in t] + results,
            in_specs=[hbm] * len(t) + [vmem] * (5 + len(moment)),
            out_specs=[hbm] * (len(t) + len(results)),
            scratch_shapes=[pltpu.VMEM((through, rows // PARTS, t[0].shape[2]), bf), dma((2, jobs))],
            compiler_params=params(2 * size * through // 2**20 + 2),
            cost_estimate=pl.CostEstimate(flops=60 * moved_bytes, bytes_accessed=moved_bytes, transcendentals=0),
            name="settle",
        )(*(pltpu.with_memory_space_constraint(one, pltpu.HBM) for one in t), own, *far, *near, *moment)

    def settled_moment(m, moment):
        layers = m[0].shape[0]
        size = 4 * sum(one.size for one in m)
        return pl.pallas_call(
            functools.partial(settle_moment, layers),
            out_shape=[like(one) for one in m],
            in_specs=[vmem] * 2,
            out_specs=[hbm] * 3,
            scratch_shapes=[dma((2, len(pieces_of(layers))))],
            compiler_params=params(16),
            cost_estimate=pl.CostEstimate(flops=60 * size, bytes_accessed=size, transcendentals=0),
            name="settle_moment",
        )(*moment)

    def completed(results, came, rows):
        layers = results[0].shape[0]
        return pl.pallas_call(
            functools.partial(complete, n, layers, rows),
            out_shape=[like(one) for one in results],
            in_specs=[hbm] * 3 + [vmem] * 8,
            out_specs=[hbm] * 3,
            scratch_shapes=[dma((2, CORES * len(pieces_of(layers))))],
            input_output_aliases={i: i for i in range(3)},
            compiler_params=params(16),
            name="complete",
        )(*results, *came)

    def step(*arrays):
        terms, weights, m, v = (arrays[i : i + 3] for i in (0, 3, 6, 9))
        out = summed(terms, weights, m, v)
        t = out[:3]
        new_m, new_v, own = (out[i : i + 2] for i in (5, 7, 9))
        far, near = (out[11], out[13], out[12], out[14]), (out[15], out[17], out[16], out[18])
        onward = [(i, (i + CORES) % devices) for i in range(devices)]
        back = [(b, a) for a, b in onward]
        other = [(i, i + 1 - 2 * (i % CORES)) for i in range(devices)]

        def hop(k):
            return [lax.ppermute(one, "dp", way) for one, way in zip(far[k : k + 2], (onward, back), strict=True)]

        def cross(came):
            return came + [lax.ppermute(one, "dp", other) for one in came]

        wide = hop(0)
        down = hop(2)
        new_g, new_u, *ms = settled((0, 1), t[:2], own[0], far[:2], near[:2], m, new_m)
        (new_d,) = settled((2,), t[2:], own[1], far[2:], near[2:], m)
        vs = settled_moment(v, new_v)
        wide = cross(wide)
        down = cross(down)
        whole = completed((new_g, new_u, new_d), wide + down, [one.shape[1] for one in m])
        return (*whole, *ms, *vs)

    all_of, cut = P(None, None, None), P(None, "dp", None)
    return jax.shard_map(
        step,
        mesh=mesh,
        in_specs=(P(("rep", "dp"), None, None, None),) * 3 + (all_of,) * 3 + (cut,) * 6,
        out_specs=(P("rep", None, None),) * 3 + (P("rep", "dp", None),) * 6,
        check_vma=False,
    )
```

time: 552 us -> 546 us (0.989)
  local copies, waits for them, and re-layouts: 47.2 us -> 0 us
  waiting for transfers between devices: 0 us -> 29.7 us
  starting transfers between devices: 0 us -> 8.45 us
    unnamed x31 -> x0, local copies, waits for them, and re-layouts: 47.2 us -> none
    ppermute x0 -> x8, waiting for transfers between devices: none -> 29.7 us  [the longest x4 29.7 us: hop(): lax.ppermute(one, 'dp', way)]
    ppermute x0 -> x8, starting transfers between devices: none -> 8.45 us  [the longest x4 5.45 us: hop(): lax.ppermute(one, 'dp', way)]
    pallas_call x1 -> x5, Pallas kernels: 503 us -> 506 us  [the longest x1 468 us: summed(): pl.pallas_call(functools.partial(kernel, n, devices * sum((one.size for o...]
  transfers between devices with their start and end apart: 0 -> 8, of which waited for: 0 -> 2; matrix products, arithmetic and copies ran while one was open for 0% -> 0% of each run, Pallas kernels for 0% -> 6%
where the time goes in v3:
time: 546 us; the launch traced here: 545 us
  Pallas kernels  506 us (93%)
  waiting for transfers between devices  29.7 us (5%)
  starting transfers between devices  8.45 us (2%)
    pallas_call x1, Pallas kernels, summed(): pl.pallas_call(functools.partial(kernel, n, devices * sum((one.size for o...  468 us
    pallas_call x2, Pallas kernels, settled(): pl.pallas_call(functools.partial(settle, n, layers, arrays, rows, bool(mo...  32.1 us
    ppermute x4, waiting for transfers between devices, hop(): lax.ppermute(one, 'dp', way)  29.7 us
  transfers between devices with their start and end apart: 8, of which 2 were waited for; matrix products, arithmetic and copies ran while one was open for 0% of the time, Pallas kernels for 6%

profile of v3, /device:TPU:21, one launch (start us, length us, event | category | flops | bytes accessed | tf_op | source)
XLA Modules:
  0.0 545.3 jit_solution(17612657482691200587)
XLA Ops:
  0.6 468.3 %summed.1 = (bf16[2,512,8192]{2,1,0:T(8,128)(2,1)}, bf16[2,512,8192]{2,1,0:T(8,128)(2,1)}, bf16[2,8192,512]{2,1,0:T(8,128)(2,1)}, bf16[64,16,8192]{2,1,0:T(8,128...) custom-call(bf16[1,2,512,8192]{3,2,1,0:T(8,128)(2,1)} %refs_0_.1, ...), custom_call_target="tpu_custom_call" | custom-call | tf_op jit(solution)/shard_map/summed/pallas_call | solution.py:419
  468.9 0.6 collective-permute-start
  469.5 2.2 collective-permute-start.1
  471.7 0.0 collective-permute-start.4
  471.7 2.7 collective-permute-start.5
  474.4 20.3 %collective-permute-done.refs_3_ = bf16[4,16,8192]{2,1,0:T(8,128)(2,1)S(1)} collective-permute-done((bf16[4,16,8192]{2,1,0:T(8,128)(2,1)S(1)}, bf16[4,16,8192]{2,1,0:T(8,128)(2,1)S(1)}, u32[]{:S(2)}, u32[]{:S(2)}) %collective-permute-start) | collective-permute-done | bytes 1048608 | tf_op jit(solution)/shard_map/ppermute | solution.py:495
  494.7 1.9 collective-permute-start.2
  496.5 0.0 collective-permute-done.1.refs_4_
  496.5 0.0 collective-permute-start.3
  496.5 9.4 %collective-permute-done.4.refs_7_ = bf16[2,256,512]{2,1,0:T(8,128)(2,1)S(1)} collective-permute-done((bf16[2,256,512]{2,1,0:T(8,128)(2,1)S(1)}, bf16[2,256,512]{2,1,0:T(8,128)(2,1)S(1)}, u32[]{:S(2)}, u32[]{:S(2)}) %collective-permute-start.4) | collective-permute-done | bytes 524320 | tf_op jit(solution)/shard_map/ppermute | solution.py:495
  505.9 1.1 collective-permute-start.6
  507.0 0.0 collective-permute-done.5.refs_8_
  507.0 0.0 collective-permute-start.7
  507.0 2.9 settle_moment.1
  509.9 10.2 %settle.3.refs_2_ = bf16[2,8192,512]{2,1,0:T(8,128)(2,1)} custom-call(bf16[2,8192,512]{2,1,0:T(8,128)(2,1)} %get-tuple-element.48.refs_0_, bf16[4,256,512]{2,1,0:T(8,128)(2,1)S(1)} %get-tuple-element.49.refs_1_, bf16[2,256,512]{2,1,0:T(8,128)(2,1)S(1)} %get-tuple-element.50.refs_2_, bf16[2,256,512]{2,1,0:T(8,128)(2,1)S(1)} %get-tuple-element.51.refs_3_, ...), custom_call_target="tpu_custom_call" | custom-call | flops 1572864000 | bytes 26214400 | tf_op jit(solution)/shard_map/settle/pallas_call | solution.py:446
  520.2 21.9 %settle.2 = (bf16[2,512,8192]{2,1,0:T(8,128)(2,1)}, bf16[2,512,8192]{2,1,0:T(8,128)(2,1)}, f32[2,32,8192]{2,1,0:T(8,128)}, f32[2,32,8192]{2,1,0:T(8,128)}, f32[2,512,512]{2,1,0:T(8,128)}) custom-call(bf16[2,512,8192]{2,1,0:T(8,128)(2,1)} %get-tuple-element.37.refs_0_, bf16[2,512,8192]{2,1,0:T(8,128)(2,1)} %get-tuple-element.38.refs_1_, ...), custom_call_target="tpu_custom_call" | custom-call | flops 3334471680 | bytes 55574528 | tf_op jit(solution)/shard_map/settle/pallas_call | solution.py:446
  542.1 0.0 collective-permute-done.6.refs_9_
  542.1 0.0 collective-permute-done.7.refs_10_
  542.1 0.0 collective-permute-done.2.refs_5_
  542.1 0.0 collective-permute-done.3.refs_6_
  542.1 3.1 complete.1
Async XLA Ops:
  468.9 25.8 %collective-permute-start = (bf16[4,16,8192]{2,1,0:T(8,128)(2,1)S(1)}, bf16[4,16,8192]{2,1,0:T(8,128)(2,1)S(1)}, u32[]{:S(2)}, u32[]{:S(2)}) collective-permute-start(bf16[4,16,8192]{2,1,0:T(8,128)(2,1)S(1)} %get-tuple-element.40.refs_3_), channel_id=1, source_target_pairs={{0,2},{1,3},{2,4},{3,5},{4,6},{5,7},{6,8},{7,9},{8,10},{9,11},{10,... | collective-permute-start | bytes 3145736 | tf_op jit(solution)/shard_map/ppermute | solution.py:495
  469.5 27.0 %collective-permute-start.1 = (bf16[4,16,8192]{2,1,0:T(8,128)(2,1)S(1)}, bf16[4,16,8192]{2,1,0:T(8,128)(2,1)S(1)}, u32[]{:S(2)}, u32[]{:S(2)}) collective-permute-start(bf16[4,16,8192]{2,1,0:T(8,128)(2,1)S(1)} %get-tuple-element.41.refs_4_), channel_id=1, source_target_pairs={{2,0},{3,1},{4,2},{5,3},{6,4},{7,5},{8,6},{9,7},{10,8},{11,9},{12,... | collective-permute-start | bytes 3145736 | tf_op jit(solution)/shard_map/ppermute | solution.py:495
  471.7 34.2 %collective-permute-start.4 = (bf16[2,256,512]{2,1,0:T(8,128)(2,1)S(1)}, bf16[2,256,512]{2,1,0:T(8,128)(2,1)S(1)}, u32[]{:S(2)}, u32[]{:S(2)}) collective-permute-start(bf16[2,256,512]{2,1,0:T(8,128)(2,1)S(1)} %get-tuple-element.50.refs_2_), channel_id=1, source_target_pairs={{0,2},{1,3},{2,4},{3,5},{4,6},{5,7},{6,8},{7,9},{8,10},{9,11},{10,... | collective-permute-start | bytes 1572872 | tf_op jit(solution)/shard_map/ppermute | solution.py:495
  471.7 35.3 %collective-permute-start.5 = (bf16[2,256,512]{2,1,0:T(8,128)(2,1)S(1)}, bf16[2,256,512]{2,1,0:T(8,128)(2,1)S(1)}, u32[]{:S(2)}, u32[]{:S(2)}) collective-permute-start(bf16[2,256,512]{2,1,0:T(8,128)(2,1)S(1)} %get-tuple-element.51.refs_3_), channel_id=1, source_target_pairs={{2,0},{3,1},{4,2},{5,3},{6,4},{7,5},{8,6},{9,7},{10,8},{11,9},{12,... | collective-permute-start | bytes 1572872 | tf_op jit(solution)/shard_map/ppermute | solution.py:495
  494.7 47.4 %collective-permute-start.2 = (bf16[4,16,8192]{2,1,0:T(8,128)(2,1)S(1)}, bf16[4,16,8192]{2,1,0:T(8,128)(2,1)S(1)}, u32[]{:S(2)}, u32[]{:S(2)}) collective-permute-start(bf16[4,16,8192]{2,1,0:T(8,128)(2,1)S(1)} %collective-permute-done.refs_3_), channel_id=1, source_target_pairs={{0,1},{1,0},{2,3},{3,2},{4,5},{5,4},{6,7},{7,6},{8,9},{9,8},{10,11... | collective-permute-start | bytes 3145736 | tf_op jit(solution)/shard_map/ppermute | solution.py:498
  496.5 45.6 %collective-permute-start.3 = (bf16[4,16,8192]{2,1,0:T(8,128)(2,1)S(1)}, bf16[4,16,8192]{2,1,0:T(8,128)(2,1)S(1)}, u32[]{:S(2)}, u32[]{:S(2)}) collective-permute-start(bf16[4,16,8192]{2,1,0:T(8,128)(2,1)S(1)} %collective-permute-done.1.refs_4_), channel_id=1, source_target_pairs={{0,1},{1,0},{2,3},{3,2},{4,5},{5,4},{6,7},{7,6},{8,9},{9,8},{10,11... | collective-permute-start | bytes 3145736 | tf_op jit(solution)/shard_map/ppermute | solution.py:498
  505.9 36.2 %collective-permute-start.6 = (bf16[2,256,512]{2,1,0:T(8,128)(2,1)S(1)}, bf16[2,256,512]{2,1,0:T(8,128)(2,1)S(1)}, u32[]{:S(2)}, u32[]{:S(2)}) collective-permute-start(bf16[2,256,512]{2,1,0:T(8,128)(2,1)S(1)} %collective-permute-done.4.refs_7_), channel_id=1, source_target_pairs={{0,1},{1,0},{2,3},{3,2},{4,5},{5,4},{6,7},{7,6},{8,9},{9,8},{10,11... | collective-permute-start | bytes 1572872 | tf_op jit(solution)/shard_map/ppermute | solution.py:498
  507.0 35.0 %collective-permute-start.7 = (bf16[2,256,512]{2,1,0:T(8,128)(2,1)S(1)}, bf16[2,256,512]{2,1,0:T(8,128)(2,1)S(1)}, u32[]{:S(2)}, u32[]{:S(2)}) collective-permute-start(bf16[2,256,512]{2,1,0:T(8,128)(2,1)S(1)} %collective-permute-done.5.refs_8_), channel_id=1, source_target_pairs={{0,1},{1,0},{2,3},{3,2},{4,5},{5,4},{6,7},{7,6},{8,9},{9,8},{10,11... | collective-permute-start | bytes 1572872 | tf_op jit(solution)/shard_map/ppermute | solution.py:498

commit v4 on v3

--- a/solution.py
+++ b/solution.py
@@ -66,13 +66,37 @@
     return items, finals, arrives, fresh, count
 
 
+def grouped(number, size, alone):
+    of, lengths = [], []
+    for k in range(number):
+        if k < number - alone and k % size:
+            lengths[-1] += 1
+        else:
+            lengths.append(1)
+        of.append(len(lengths) - 1)
+    return of, lengths
+
+
+def groups_of(n, layers):
+    items, finals, _, _, _ = plan(n, layers)
+    pieces = len(pieces_of(layers))
+    ring = grouped(len(items) // 2, 3, 3)
+    of, lengths = grouped(len(items) + len(finals), 6, 6)
+    terms = [len(lengths) - 1 - k for k in reversed(of)], lengths[::-1]
+    return ring, terms, grouped((n // 2 - 1) * pieces, 3, 3)
+
+
+def waited(ref, sem):
+    pltpu.make_async_copy(ref, ref, sem).wait()
+
+
 def kernel(n, count_all, *refs):
     g, w, m, v, t = (refs[i : i + 3] for i in range(0, 15, 3))
     xs, ms, vs, own_new = (refs[i : i + 2] for i in range(15, 23, 2))
     far = {way: refs[23 + 2 * way : 25 + 2 * way] for way in WAYS}
     near = {way: refs[27 + 2 * way : 29 + 2 * way] for way in WAYS}
     landed, st_own, st_other, old = (refs[i : i + 2] for i in range(31, 39, 2))
-    squares, rs_send, rs_recv, x_send, x_recv, st_sem, ag_send, ag_recv, y_send, y_recv, sq_send, sq_recv, in_sem, _ = refs[39:]
+    squares, rs_send, rs_recv, x_send, x_recv, st_sem, ag_send, ag_recv, y_send, y_recv, sq_send, sq_recv, in_sem = refs[39:]
 
     layers = m[0].shape[0]
     rows = [a.shape[1] for a in m]
@@ -81,6 +105,14 @@
     todo = items + finals
     half = n // 2
     devices = n * CORES
+    ring_groups, term_groups, gather_groups = groups_of(n, layers)
+    met = set()
+
+    def arrive(name, sem, groups, way, k):
+        of, lengths = groups
+        if (name, way, of[k]) not in met:
+            met.add((name, way, of[k]))
+            waited(landed[0].at[pl.ds(0, lengths[of[k]])], sem.at[way * len(lengths) + of[k]])
 
     me = lax.axis_index("dp")
     z, c = me // CORES, me % CORES
@@ -122,7 +154,7 @@
     def exchange(i):
         way, d, q = todo[i]
         kind, k = x_at[i]
-        return remote(term(q, at(target(way, d), 1 - c)), xs[kind].at[k], x_send.at[i], x_recv.at[i], partner)
+        return remote(term(q, at(target(way, d), 1 - c)), xs[kind].at[k], x_send.at[kind], x_recv.at[term_groups[0][i]], partner)
 
     def stage(i):
         way, d, q = todo[i]
@@ -135,7 +167,7 @@
         )
 
     def stage_start(i):
-        exchange(i).wait_recv()
+        arrive("term", x_recv, term_groups, 0, i)
         for copy in stage(i):
             copy.start()
 
@@ -171,16 +203,19 @@
         way, d, q = s
         kind, k = fresh[s] if s in fresh else arrives[(way, d + 1, q)]
         to_kind, to = arrives[s]
-        i = items.index(s)
-        return remote(landed[kind].at[k], landed[to_kind].at[to], rs_send.at[i], rs_recv.at[i], ahead[way])
+        group = way * len(ring_groups[1]) + ring_groups[0][items.index(s) // 2]
+        return remote(landed[kind].at[k], landed[to_kind].at[to], rs_send.at[kind], rs_recv.at[group], ahead[way])
+
+    def ring_arrive(s):
+        arrive("ring", rs_recv, ring_groups, s[0], items.index(s) // 2)
 
     def load_state(e):
         q = pieces[e]
         part = (q[1], pl.ds(q[2] * (rows[q[0]] // PARTS), rows[q[0]] // PARTS))
         return (
-            pltpu.make_async_copy(m[q[0]].at[part], kept(ms, q), in_sem.at[0, e]),
-            pltpu.make_async_copy(v[q[0]].at[part], kept(vs, q), in_sem.at[1, e]),
-            pltpu.make_async_copy(block(w, q, me), kept(old, q), in_sem.at[2, e]),
+            pltpu.make_async_copy(m[q[0]].at[part], kept(ms, q), in_sem.at[0, kind_of(q)]),
+            pltpu.make_async_copy(v[q[0]].at[part], kept(vs, q), in_sem.at[1, kind_of(q)]),
+            pltpu.make_async_copy(block(w, q, me), kept(old, q), in_sem.at[2, kind_of(q)]),
         )
 
     window, reach = 24, 3
@@ -197,7 +232,7 @@
         terms = [st_own[kind].at[k % depth[kind]], st_other[kind].at[k % depth[kind]]]
         if way is not None:
             if s not in fresh:
-                ring((way, d + 1, q)).wait_recv()
+                ring_arrive((way, d + 1, q))
                 kind, k = arrives[(way, d + 1, q)]
                 terms.append(landed[kind].at[k])
             else:
@@ -206,7 +241,7 @@
             ring(s).start()
         else:
             for from_ in WAYS:
-                ring((from_, 1, q)).wait_recv()
+                ring_arrive((from_, 1, q))
                 kind, k = arrives[(from_, 1, q)]
                 terms.append(landed[kind].at[k])
             total = added(kept(own_new, q), terms, kind, total)
@@ -220,21 +255,20 @@
 
     squares[me] = total
 
-    def share(j, sender):
-        to = lax.rem(me + j, devices)
-        return remote(squares.at[sender], squares.at[sender], sq_send.at[j - 1], sq_recv.at[j - 1], to)
+    def share(j):
+        return remote(squares.at[me], squares.at[me], sq_send.at[0], sq_recv.at[0], lax.rem(me + j, devices))
+
+    def several(number, ref):
+        return ref.at[pl.ds(0, number)]
 
     for j in range(1, devices):
-        share(j, me).start()
-    for i in range(len(todo)):
-        exchange(i).wait_send()
-    for s in items:
-        ring(s).wait_send()
-    for e in range(len(pieces)):
-        for copy in load_state(e):
-            copy.wait()
-    for j in range(1, devices):
-        share(j, lax.rem(me - j + devices, devices)).wait_recv()
+        share(j).start()
+    for kind in (0, 1):
+        waited(xs[kind], x_send.at[kind])
+        waited(several(sum(kind_of(s[2]) == kind for s in items), landed[kind]), rs_send.at[kind])
+        for which, pair in enumerate((ms, vs, old)):
+            waited(pair[kind], in_sem.at[which, kind])
+    waited(several(devices - 1, squares), sq_recv.at[0])
     everyone = jnp.sum(jnp.sum(squares[...], axis=0), axis=(0, 1), keepdims=True)
     factor = jnp.minimum(1.0, 0.5 * lax.rsqrt(jnp.broadcast_to(everyone, (8, 128)) / count_all + 1e-30))[0:1, 0:1]
 
@@ -264,61 +298,56 @@
         kind, k = place(q, among)
         return which[way][kind].at[k]
 
-    def pass_on(s, arriving):
+    def pass_on(s):
         way, h, q = s
-        owner = at(z - step[way] * (h if arriving else h - 1), c)
-        i = gathers.index(s)
-        src = kept(own_new, q) if h == 1 and not arriving else block(t, q, owner)
-        return remote(src, lies(way, h, q, owner), ag_send.at[i], ag_recv.at[i], ahead[way])
-
-    def across(i, arriving):
-        core = 1 - c if arriving else c
-        if i < len(gathers):
-            way, h, q = gathers[i]
-            owner = at(z - step[way] * h, core)
-            src = lies(way, h, q, owner)
-        else:
-            q = pieces[i - len(gathers)]
-            owner = at(z, core)
-            src = kept(own_new, q)
-        return remote(src, block(t, q, owner), y_send.at[i], y_recv.at[i], partner)
-
-    for e, q in enumerate(pieces):
+        owner = at(z - step[way] * (h - 1), c)
+        group = way * len(gather_groups[1]) + gather_groups[0][gathers.index(s) // 2]
+        src = kept(own_new, q) if h == 1 else block(t, q, owner)
+        return remote(src, lies(way, h, q, owner), ag_send.at[kind_of(q)], ag_recv.at[group], ahead[way])
+
+    def across(q, owner, src):
+        return remote(src, block(t, q, owner), y_send.at[kind_of(q)], y_recv.at[kind_of(q)], partner)
+
+    for q in pieces:
         stepped(q)
         for way in WAYS:
-            pass_on((way, 1, q), False).start()
-        across(len(gathers) + e, False).start()
+            pass_on((way, 1, q)).start()
+        across(q, me, kept(own_new, q)).start()
     for i, s in enumerate(gathers):
         way, h, q = s
-        pass_on(s, True).wait_recv()
+        owner = at(z - step[way] * h, c)
+        arrive("gather", ag_recv, gather_groups, way, i // 2)
         if h + 1 < half:
-            pass_on((way, h + 1, q), False).start()
-        across(i, False).start()
-    for j in range(1, devices):
-        share(j, me).wait_send()
-    for s in gathers:
-        pass_on(s, False).wait_send()
-    for i in range(len(gathers) + len(pieces)):
-        across(i, False).wait_send()
-    for i in range(len(gathers) + len(pieces)):
-        across(i, True).wait_recv()
-
-
-def moved(jobs, sem):
-    ins = [pltpu.make_async_copy(a, b, sem.at[0, j]) if b is not None else None for j, (a, b, _) in enumerate(jobs)]
-    outs = [pltpu.make_async_copy(a if b is None else b, c, sem.at[1, j]) for j, (a, b, c) in enumerate(jobs)]
-    for copy in ins:
-        if copy is not None:
-            copy.start()
-    for copy, then in zip(ins, outs, strict=True):
-        if copy is None:
-            then.start()
-    for copy, then in zip(ins, outs, strict=True):
-        if copy is not None:
-            copy.wait()
-            then.start()
-    for copy in outs:
-        copy.wait()
+            pass_on((way, h + 1, q)).start()
+        across(q, owner, lies(way, h, q, owner)).start()
+    waited(several(devices - 1, squares), sq_send.at[0])
+    for kind in (0, 1):
+        number = sum(kind_of(s[2]) == kind for s in gathers)
+        waited(several(number, landed[kind]), ag_send.at[kind])
+        number += sum(kind_of(q) == kind for q in pieces)
+        waited(several(number, landed[kind]), y_send.at[kind])
+        waited(several(number, landed[kind]), y_recv.at[kind])
+
+
+READS = 4
+
+
+def moved(sem, through=(), buf=None, direct=()):
+    reads = -(-len(through) // READS)
+    for j, (a, _) in enumerate(through):
+        pltpu.make_async_copy(a, buf.at[j], sem.at[j // READS]).start()
+    for k, (copies, _) in enumerate(direct):
+        for a, b in copies:
+            pltpu.make_async_copy(a, b, sem.at[reads + 1 + k]).start()
+    for i in range(reads):
+        these = range(i * READS, min(len(through), (i + 1) * READS))
+        waited(buf.at[pl.ds(i * READS, len(these))], sem.at[i])
+        for j in these:
+            pltpu.make_async_copy(buf.at[j], through[j][1], sem.at[reads]).start()
+    if through:
+        waited(buf, sem.at[reads])
+    for k, (_, total) in enumerate(direct):
+        waited(total, sem.at[reads + 1 + k])
 
 
 def row_part(ref, layer, part, rows, owner):
@@ -326,15 +355,15 @@
     return ref.at[layer, pl.ds(pl.multiple_of(owner * rows + part * size, size), size)]
 
 
-def moment_jobs(pair, results, layers):
+def moment_copies(pair, results, layers):
     pieces = pieces_of(layers)
-    jobs = []
+    sets = [([], pair[0]), ([], pair[1])]
     for q in pieces:
         a, layer, part = q
         kind, k = place(q, pieces)
         size = results[a].shape[1] // PARTS
-        jobs.append((pair[kind].at[k], None, results[a].at[layer, pl.ds(part * size, size)]))
-    return jobs
+        sets[kind][0].append((pair[kind].at[k], results[a].at[layer, pl.ds(part * size, size)]))
+    return sets
 
 
 def settle(n, layers, arrays, rows, moment, *refs):
@@ -349,8 +378,7 @@
     me = lax.axis_index("dp")
     z, c = me // CORES, me % CORES
     pieces = pieces_of(layers)
-    jobs = moment_jobs(pair, results, layers) if moment else []
-    through = 0
+    through, held = [], []
     for off in range(n):
         if off == half:
             continue
@@ -369,29 +397,29 @@
                         which, among = (far, far_half(way, layers)) if q in far_half(way, layers) else (near, half_of(way, layers))
                         src = which[way].at[place(q, among)[1]]
                 if src is not None:
-                    jobs.append((src, None, dst))
+                    held.append((src, dst))
                 else:
-                    jobs.append((row_part(t[arrays.index(a)], layer, part, rows, owner), buf.at[through], dst))
-                    through += 1
-    moved(jobs, sem)
+                    through.append((row_part(t[arrays.index(a)], layer, part, rows, owner), dst))
+    direct = [(held, buf.at[pl.ds(0, len(held))])] + (moment_copies(pair, results, layers) if moment else [])
+    moved(sem, through, buf, direct)
 
 
 def settle_moment(layers, *refs):
-    moved(moment_jobs(refs[:2], refs[2:5], layers), refs[5])
+    moved(refs[5], direct=moment_copies(refs[:2], refs[2:5], layers))
 
 
 def complete(n, layers, rows, *refs):
     came, outs, sem = refs[3:11], refs[11:14], refs[14]
     me = lax.axis_index("dp")
     z, c = me // CORES, me % CORES
-    jobs = []
+    copies = []
     for core in range(CORES):
         owner = lax.rem(z + n // 2, n) * CORES + (c if core == 0 else 1 - c)
         for way in WAYS:
             for q in far_half(way, layers):
                 kind, k = place(q, far_half(way, layers))
-                jobs.append((came[4 * kind + 2 * core + way].at[k], None, row_part(outs[q[0]], q[1], q[2], rows[q[0]], owner)))
-    moved(jobs, sem)
+                copies.append((came[4 * kind + 2 * core + way].at[k], row_part(outs[q[0]], q[1], q[2], rows[q[0]], owner)))
+    moved(sem, direct=[(copies, outs[0].at[0, pl.ds(0, len(copies) * (rows[0] // PARTS))])])
 
 
 def solution(mesh):
@@ -413,7 +441,7 @@
         shapes = [(m[a].shape[1] // PARTS, m[a].shape[2]) for a in (0, DOWN)]
         pair = lambda make, number, dtype: [make((number[kind], *shapes[kind]), dtype) for kind in (0, 1)]
         whole, part = counts(pieces), counts(half_of(PLUS, layers))
-        hops = 2 * (n // 2 - 1) * len(pieces)
+        ring_groups, term_groups, gather_groups = groups_of(n, layers)
         outs = [like(w) for w in weights] + pair(jax.ShapeDtypeStruct, counts([s[2] for s in todo]), bf)
         held = 2 * pair(pltpu.VMEM, whole, f32) + pair(pltpu.VMEM, whole, bf) + 4 * pair(pltpu.VMEM, part, bf)
         return pl.pallas_call(
@@ -425,13 +453,13 @@
             + 2 * pair(pltpu.VMEM, (4, 2), bf)
             + pair(pltpu.VMEM, whole, bf)
             + [pltpu.VMEM((devices, 8, 128), f32)]
-            + [dma((len(items),))] * 2
-            + [dma((len(todo),))] * 2
+            + [dma((2,)), dma((2 * len(ring_groups[1]),))]
+            + [dma((2,)), dma((len(term_groups[1]),))]
             + [dma((2, 6))]
-            + [dma((hops,))] * 2
-            + [dma((hops + len(pieces),))] * 2
-            + [dma((devices - 1,))] * 2
-            + [dma((3, len(pieces)))] * 2,
+            + [dma((2,)), dma((2 * len(gather_groups[1]),))]
+            + [dma((2,)), dma((2,))]
+            + [dma((1,)), dma((1,))]
+            + [dma((3, 2))],
             compiler_params=params(38, collective_id=0, has_side_effects=True),
             name="summed",
         )(*terms, *weights, *m, *v)
@@ -448,7 +476,7 @@
             out_shape=[like(one) for one in t] + results,
             in_specs=[hbm] * len(t) + [vmem] * (5 + len(moment)),
             out_specs=[hbm] * (len(t) + len(results)),
-            scratch_shapes=[pltpu.VMEM((through, rows // PARTS, t[0].shape[2]), bf), dma((2, jobs))],
+            scratch_shapes=[pltpu.VMEM((through, rows // PARTS, t[0].shape[2]), bf), dma((-(-through // READS) + 4,))],
             compiler_params=params(2 * size * through // 2**20 + 2),
             cost_estimate=pl.CostEstimate(flops=60 * moved_bytes, bytes_accessed=moved_bytes, transcendentals=0),
             name="settle",
@@ -462,7 +490,7 @@
             out_shape=[like(one) for one in m],
             in_specs=[vmem] * 2,
             out_specs=[hbm] * 3,
-            scratch_shapes=[dma((2, len(pieces_of(layers))))],
+            scratch_shapes=[dma((3,))],
             compiler_params=params(16),
             cost_estimate=pl.CostEstimate(flops=60 * size, bytes_accessed=size, transcendentals=0),
             name="settle_moment",
@@ -475,7 +503,7 @@
             out_shape=[like(one) for one in results],
             in_specs=[hbm] * 3 + [vmem] * 8,
             out_specs=[hbm] * 3,
-            scratch_shapes=[dma((2, CORES * len(pieces_of(layers))))],
+            scratch_shapes=[dma((2,))],
             input_output_aliases={i: i for i in range(3)},
             compiler_params=params(16),
             name="complete",

time: 546 us -> 537 us (0.984)
  Pallas kernels: 506 us -> 497 us
    pallas_call x1, Pallas kernels: 468 us -> 462 us  [summed(): pl.pallas_call(functools.partial(kernel, n, devices * sum((one.size for o...]
where the time goes in v4:
time: 537 us; the launch traced here: 536 us
  Pallas kernels  497 us (93%)
  waiting for transfers between devices  30.1 us (6%)
  starting transfers between devices  8.05 us (1%)
    pallas_call x1, Pallas kernels, summed(): pl.pallas_call(functools.partial(kernel, n, devices * sum((one.size for o...  462 us
    ppermute x4, waiting for transfers between devices, hop(): lax.ppermute(one, 'dp', way)  30.1 us
    pallas_call x2, Pallas kernels, settled(): pl.pallas_call(functools.partial(settle, n, layers, arrays, rows, bool(mo...  29.6 us
  transfers between devices with their start and end apart: 8, of which 2 were waited for; matrix products, arithmetic and copies ran while one was open for 0% of the time, Pallas kernels for 6%

profile of v4, /device:TPU:21, one launch (start us, length us, event | category | flops | bytes accessed | tf_op | source)
XLA Modules:
  0.0 536.0 jit_solution(354465788813227902)
XLA Ops:
  0.6 462.2 %summed.1 = (bf16[2,512,8192]{2,1,0:T(8,128)(2,1)}, bf16[2,512,8192]{2,1,0:T(8,128)(2,1)}, bf16[2,8192,512]{2,1,0:T(8,128)(2,1)}, bf16[64,16,8192]{2,1,0:T(8,128...) custom-call(bf16[1,2,512,8192]{3,2,1,0:T(8,128)(2,1)} %refs_0_.1, ...), custom_call_target="tpu_custom_call" | custom-call | tf_op jit(solution)/shard_map/summed/pallas_call | solution.py:447
  462.8 0.6 collective-permute-start
  463.5 2.2 collective-permute-start.1
  465.6 0.0 collective-permute-start.4
  465.6 2.7 collective-permute-start.5
  468.3 20.4 %collective-permute-done.refs_3_ = bf16[4,16,8192]{2,1,0:T(8,128)(2,1)S(1)} collective-permute-done((bf16[4,16,8192]{2,1,0:T(8,128)(2,1)S(1)}, bf16[4,16,8192]{2,1,0:T(8,128)(2,1)S(1)}, u32[]{:S(2)}, u32[]{:S(2)}) %collective-permute-start) | collective-permute-done | bytes 1048608 | tf_op jit(solution)/shard_map/ppermute | solution.py:523
  488.7 1.6 collective-permute-start.2
  490.3 0.0 collective-permute-done.1.refs_4_
  490.3 0.0 collective-permute-start.3
  490.3 9.6 %collective-permute-done.4.refs_7_ = bf16[2,256,512]{2,1,0:T(8,128)(2,1)S(1)} collective-permute-done((bf16[2,256,512]{2,1,0:T(8,128)(2,1)S(1)}, bf16[2,256,512]{2,1,0:T(8,128)(2,1)S(1)}, u32[]{:S(2)}, u32[]{:S(2)}) %collective-permute-start.4) | collective-permute-done | bytes 524320 | tf_op jit(solution)/shard_map/ppermute | solution.py:523
  500.0 1.0 collective-permute-start.6
  501.0 0.0 collective-permute-done.5.refs_8_
  501.0 0.0 collective-permute-start.7
  501.0 2.7 settle_moment.1
  503.6 9.8 %settle.3.refs_2_ = bf16[2,8192,512]{2,1,0:T(8,128)(2,1)} custom-call(bf16[2,8192,512]{2,1,0:T(8,128)(2,1)} %get-tuple-element.48.refs_0_, bf16[4,256,512]{2,1,0:T(8,128)(2,1)S(1)} %get-tuple-element.49.refs_1_, bf16[2,256,512]{2,1,0:T(8,128)(2,1)S(1)} %get-tuple-element.50.refs_2_, bf16[2,256,512]{2,1,0:T(8,128)(2,1)S(1)} %get-tuple-element.51.refs_3_, ...), custom_call_target="tpu_custom_call" | custom-call | flops 1572864000 | bytes 26214400 | tf_op jit(solution)/shard_map/settle/pallas_call | solution.py:474
  513.4 19.9 %settle.2 = (bf16[2,512,8192]{2,1,0:T(8,128)(2,1)}, bf16[2,512,8192]{2,1,0:T(8,128)(2,1)}, f32[2,32,8192]{2,1,0:T(8,128)}, f32[2,32,8192]{2,1,0:T(8,128)}, f32[2,512,512]{2,1,0:T(8,128)}) custom-call(bf16[2,512,8192]{2,1,0:T(8,128)(2,1)} %get-tuple-element.37.refs_0_, bf16[2,512,8192]{2,1,0:T(8,128)(2,1)} %get-tuple-element.38.refs_1_, ...), custom_call_target="tpu_custom_call" | custom-call | flops 3334471680 | bytes 55574528 | tf_op jit(solution)/shard_map/settle/pallas_call | solution.py:474
  533.3 0.0 collective-permute-done.6.refs_9_
  533.3 0.0 collective-permute-done.7.refs_10_
  533.3 0.0 collective-permute-done.2.refs_5_
  533.3 0.0 collective-permute-done.3.refs_6_
  533.3 2.7 complete.1
Async XLA Ops:
  462.8 25.9 %collective-permute-start = (bf16[4,16,8192]{2,1,0:T(8,128)(2,1)S(1)}, bf16[4,16,8192]{2,1,0:T(8,128)(2,1)S(1)}, u32[]{:S(2)}, u32[]{:S(2)}) collective-permute-start(bf16[4,16,8192]{2,1,0:T(8,128)(2,1)S(1)} %get-tuple-element.40.refs_3_), channel_id=1, source_target_pairs={{0,2},{1,3},{2,4},{3,5},{4,6},{5,7},{6,8},{7,9},{8,10},{9,11},{10,... | collective-permute-start | bytes 3145736 | tf_op jit(solution)/shard_map/ppermute | solution.py:523
  463.5 26.9 %collective-permute-start.1 = (bf16[4,16,8192]{2,1,0:T(8,128)(2,1)S(1)}, bf16[4,16,8192]{2,1,0:T(8,128)(2,1)S(1)}, u32[]{:S(2)}, u32[]{:S(2)}) collective-permute-start(bf16[4,16,8192]{2,1,0:T(8,128)(2,1)S(1)} %get-tuple-element.41.refs_4_), channel_id=1, source_target_pairs={{2,0},{3,1},{4,2},{5,3},{6,4},{7,5},{8,6},{9,7},{10,8},{11,9},{12,... | collective-permute-start | bytes 3145736 | tf_op jit(solution)/shard_map/ppermute | solution.py:523
  465.6 34.3 %collective-permute-start.4 = (bf16[2,256,512]{2,1,0:T(8,128)(2,1)S(1)}, bf16[2,256,512]{2,1,0:T(8,128)(2,1)S(1)}, u32[]{:S(2)}, u32[]{:S(2)}) collective-permute-start(bf16[2,256,512]{2,1,0:T(8,128)(2,1)S(1)} %get-tuple-element.50.refs_2_), channel_id=1, source_target_pairs={{0,2},{1,3},{2,4},{3,5},{4,6},{5,7},{6,8},{7,9},{8,10},{9,11},{10,... | collective-permute-start | bytes 1572872 | tf_op jit(solution)/shard_map/ppermute | solution.py:523
  465.6 35.3 %collective-permute-start.5 = (bf16[2,256,512]{2,1,0:T(8,128)(2,1)S(1)}, bf16[2,256,512]{2,1,0:T(8,128)(2,1)S(1)}, u32[]{:S(2)}, u32[]{:S(2)}) collective-permute-start(bf16[2,256,512]{2,1,0:T(8,128)(2,1)S(1)} %get-tuple-element.51.refs_3_), channel_id=1, source_target_pairs={{2,0},{3,1},{4,2},{5,3},{6,4},{7,5},{8,6},{9,7},{10,8},{11,9},{12,... | collective-permute-start | bytes 1572872 | tf_op jit(solution)/shard_map/ppermute | solution.py:523
  488.7 44.6 %collective-permute-start.2 = (bf16[4,16,8192]{2,1,0:T(8,128)(2,1)S(1)}, bf16[4,16,8192]{2,1,0:T(8,128)(2,1)S(1)}, u32[]{:S(2)}, u32[]{:S(2)}) collective-permute-start(bf16[4,16,8192]{2,1,0:T(8,128)(2,1)S(1)} %collective-permute-done.refs_3_), channel_id=1, source_target_pairs={{0,1},{1,0},{2,3},{3,2},{4,5},{5,4},{6,7},{7,6},{8,9},{9,8},{10,11... | collective-permute-start | bytes 3145736 | tf_op jit(solution)/shard_map/ppermute | solution.py:526
  490.3 43.0 %collective-permute-start.3 = (bf16[4,16,8192]{2,1,0:T(8,128)(2,1)S(1)}, bf16[4,16,8192]{2,1,0:T(8,128)(2,1)S(1)}, u32[]{:S(2)}, u32[]{:S(2)}) collective-permute-start(bf16[4,16,8192]{2,1,0:T(8,128)(2,1)S(1)} %collective-permute-done.1.refs_4_), channel_id=1, source_target_pairs={{0,1},{1,0},{2,3},{3,2},{4,5},{5,4},{6,7},{7,6},{8,9},{9,8},{10,11... | collective-permute-start | bytes 3145736 | tf_op jit(solution)/shard_map/ppermute | solution.py:526
  500.0 33.3 %collective-permute-start.6 = (bf16[2,256,512]{2,1,0:T(8,128)(2,1)S(1)}, bf16[2,256,512]{2,1,0:T(8,128)(2,1)S(1)}, u32[]{:S(2)}, u32[]{:S(2)}) collective-permute-start(bf16[2,256,512]{2,1,0:T(8,128)(2,1)S(1)} %collective-permute-done.4.refs_7_), channel_id=1, source_target_pairs={{0,1},{1,0},{2,3},{3,2},{4,5},{5,4},{6,7},{7,6},{8,9},{9,8},{10,11... | collective-permute-start | bytes 1572872 | tf_op jit(solution)/shard_map/ppermute | solution.py:526
  501.0 32.3 %collective-permute-start.7 = (bf16[2,256,512]{2,1,0:T(8,128)(2,1)S(1)}, bf16[2,256,512]{2,1,0:T(8,128)(2,1)S(1)}, u32[]{:S(2)}, u32[]{:S(2)}) collective-permute-start(bf16[2,256,512]{2,1,0:T(8,128)(2,1)S(1)} %collective-permute-done.5.refs_8_), channel_id=1, source_target_pairs={{0,1},{1,0},{2,3},{3,2},{4,5},{5,4},{6,7},{7,6},{8,9},{9,8},{10,11... | collective-permute-start | bytes 1572872 | tf_op jit(solution)/shard_map/ppermute | solution.py:526

commit v5 on v4

--- a/solution.py
+++ b/solution.py
@@ -37,6 +37,10 @@
 
 def far_half(way, layers):
     return half_of(1 - way, layers)
+
+
+def late(n, way, h, q):
+    return h == n // 2 - 1 and q[0] == DOWN and q[2] == PARTS - 1
 
 
 def plan(n, layers):
@@ -81,9 +85,9 @@
     items, finals, _, _, _ = plan(n, layers)
     pieces = len(pieces_of(layers))
     ring = grouped(len(items) // 2, 3, 3)
-    of, lengths = grouped(len(items) + len(finals), 6, 6)
+    of, lengths = grouped(len(items) + len(finals), 12, 6)
     terms = [len(lengths) - 1 - k for k in reversed(of)], lengths[::-1]
-    return ring, terms, grouped((n // 2 - 1) * pieces, 3, 3)
+    return ring, terms, grouped((n // 2 - 1) * pieces, 6, 3)
 
 
 def waited(ref, sem):
@@ -138,36 +142,34 @@
     def remote(src, dst, send, recv, to):
         return pltpu.make_async_remote_copy(src_ref=src, dst_ref=dst, send_sem=send, recv_sem=recv, device_id={"dp": to}, device_id_type=MESH)
 
-    barrier = pltpu.get_barrier_semaphore()
-    for to in (partner, ahead[PLUS], ahead[MINUS]):
-        pl.semaphore_signal(barrier, inc=1, device_id={"dp": to}, device_id_type=MESH)
-    pl.semaphore_wait(barrier, 3)
-
     x_at = []
     for _, _, q in todo:
         x_at.append((kind_of(q), sum(kind == kind_of(q) for kind, _ in x_at)))
     depth = [ref.shape[0] for ref in st_own]
 
+    def early(i):
+        return x_at[i][1] < depth[x_at[i][0]]
+
     def target(way, d):
         return z if way is None else z + step[way] * d
 
     def exchange(i):
         way, d, q = todo[i]
         kind, k = x_at[i]
-        return remote(term(q, at(target(way, d), 1 - c)), xs[kind].at[k], x_send.at[kind], x_recv.at[term_groups[0][i]], partner)
+        dst = (st_other if early(i) else xs)[kind].at[k]
+        return remote(term(q, at(target(way, d), 1 - c)), dst, x_send.at[kind], x_recv.at[term_groups[0][i]], partner)
 
     def stage(i):
         way, d, q = todo[i]
         kind, k = x_at[i]
         s = k % depth[kind]
         sem = kind * depth[0] + s
-        return (
-            pltpu.make_async_copy(term(q, at(target(way, d), c)), st_own[kind].at[s], st_sem.at[0, sem]),
-            pltpu.make_async_copy(xs[kind].at[k], st_other[kind].at[s], st_sem.at[1, sem]),
-        )
+        own = pltpu.make_async_copy(term(q, at(target(way, d), c)), st_own[kind].at[s], st_sem.at[0, sem])
+        return [own] if early(i) else [own, pltpu.make_async_copy(xs[kind].at[k], st_other[kind].at[s], st_sem.at[1, sem])]
 
     def stage_start(i):
-        arrive("term", x_recv, term_groups, 0, i)
+        if not early(i):
+            arrive("term", x_recv, term_groups, 0, i)
         for copy in stage(i):
             copy.start()
 
@@ -219,14 +221,21 @@
         )
 
     window, reach = 24, 3
+    first = [i for i in range(len(todo)) if early(i)]
+    for i in first:
+        stage_start(i)
+    barrier = pltpu.get_barrier_semaphore()
+    for to in (partner, ahead[PLUS], ahead[MINUS]):
+        pl.semaphore_signal(barrier, inc=1, device_id={"dp": to}, device_id_type=MESH)
+    pl.semaphore_wait(barrier, 3)
     for i in range(window):
         exchange(i).start()
-    for i in range(reach):
-        stage_start(i)
     total = jnp.zeros((8, 128), jnp.float32)
     for i, s in enumerate(todo):
         way, d, q = s
         kind, k = x_at[i]
+        if early(i):
+            arrive("term", x_recv, term_groups, 0, i)
         for copy in stage(i):
             copy.wait()
         terms = [st_own[kind].at[k % depth[kind]], st_other[kind].at[k % depth[kind]]]
@@ -247,7 +256,7 @@
             total = added(kept(own_new, q), terms, kind, total)
         if i + window < len(todo):
             exchange(i + window).start()
-        if i + reach < len(todo):
+        if i + reach < len(todo) and not early(i + reach):
             stage_start(i + reach)
         if 12 <= i < 12 + len(pieces):
             for copy in load_state(i - 12):
@@ -261,7 +270,7 @@
     def several(number, ref):
         return ref.at[pl.ds(0, number)]
 
-    for j in range(1, devices):
+    for j in sorted(range(1, devices), key=lambda j: -min(j, devices - j)):
         share(j).start()
     for kind in (0, 1):
         waited(xs[kind], x_send.at[kind])
@@ -319,12 +328,13 @@
         arrive("gather", ag_recv, gather_groups, way, i // 2)
         if h + 1 < half:
             pass_on((way, h + 1, q)).start()
-        across(q, owner, lies(way, h, q, owner)).start()
+        if not late(n, way, h, q):
+            across(q, owner, lies(way, h, q, owner)).start()
     waited(several(devices - 1, squares), sq_send.at[0])
     for kind in (0, 1):
         number = sum(kind_of(s[2]) == kind for s in gathers)
         waited(several(number, landed[kind]), ag_send.at[kind])
-        number += sum(kind_of(q) == kind for q in pieces)
+        number += sum(kind_of(q) == kind for q in pieces) - sum(kind_of(s[2]) == kind and late(n, *s) for s in gathers)
         waited(several(number, landed[kind]), y_send.at[kind])
         waited(several(number, landed[kind]), y_recv.at[kind])
 
@@ -366,13 +376,12 @@
     return sets
 
 
-def settle(n, layers, arrays, rows, moment, *refs):
-    k = len(arrays)
-    t, own, refs = refs[:k], refs[k], refs[k + 1 :]
-    far, near, refs = refs[0:2], refs[2:4], refs[4:]
-    pair, refs = (refs[:2], refs[2:]) if moment else (None, refs)
-    outs, refs = refs[:k], refs[k:]
-    results, refs = (refs[:3], refs[3:]) if moment else (None, refs)
+def settle(n, layers, arrays, rows, moments, lates, *refs):
+    refs = list(refs)
+    take = lambda number: [refs.pop(0) for _ in range(number)]
+    t, own, far, near = take(len(arrays)), take(1)[0], take(2), take(2)
+    pairs, crossed = [take(2) for _ in range(moments)], take(lates)
+    outs, results = take(len(arrays)), [take(3) for _ in range(moments)]
     buf, sem = refs
     half = n // 2
     me = lax.axis_index("dp")
@@ -393,23 +402,25 @@
                 if core == 0 and off == 0:
                     src = own.at[place(q, pieces)[1]]
                 for way, come in ((PLUS, n - (half - 1)), (MINUS, half - 1)):
-                    if core == 0 and off == come:
+                    if off == come:
                         which, among = (far, far_half(way, layers)) if q in far_half(way, layers) else (near, half_of(way, layers))
-                        src = which[way].at[place(q, among)[1]]
+                        if core == 0:
+                            src = which[way].at[place(q, among)[1]]
+                        elif late(n, way, half - 1, q):
+                            src = crossed[way].at[place(q, among)[1]]
                 if src is not None:
                     held.append((src, dst))
                 else:
                     through.append((row_part(t[arrays.index(a)], layer, part, rows, owner), dst))
-    direct = [(held, buf.at[pl.ds(0, len(held))])] + (moment_copies(pair, results, layers) if moment else [])
+    direct = [(held, buf.at[pl.ds(0, len(held))])]
+    for pair, one in zip(pairs, results, strict=True):
+        direct += moment_copies(pair, one, layers)
     moved(sem, through, buf, direct)
 
 
-def settle_moment(layers, *refs):
-    moved(refs[5], direct=moment_copies(refs[:2], refs[2:5], layers))
-
-
-def complete(n, layers, rows, *refs):
-    came, outs, sem = refs[3:11], refs[11:14], refs[14]
+def complete(n, layers, arrays, rows, *refs):
+    k = len(arrays)
+    came, outs, sem = refs[k : k + 4], refs[k + 4 : 2 * k + 4], refs[2 * k + 4]
     me = lax.axis_index("dp")
     z, c = me // CORES, me % CORES
     copies = []
@@ -417,9 +428,10 @@
         owner = lax.rem(z + n // 2, n) * CORES + (c if core == 0 else 1 - c)
         for way in WAYS:
             for q in far_half(way, layers):
-                kind, k = place(q, far_half(way, layers))
-                copies.append((came[4 * kind + 2 * core + way].at[k], row_part(outs[q[0]], q[1], q[2], rows[q[0]], owner)))
-    moved(sem, direct=[(copies, outs[0].at[0, pl.ds(0, len(copies) * (rows[0] // PARTS))])])
+                if q[0] in arrays:
+                    src = came[2 * core + way].at[place(q, far_half(way, layers))[1]]
+                    copies.append((src, row_part(outs[arrays.index(q[0])], q[1], q[2], rows, owner)))
+    moved(sem, direct=[(copies, outs[0].at[0, pl.ds(0, len(copies) * (rows // PARTS))])])
 
 
 def solution(mesh):
@@ -460,51 +472,38 @@
             + [dma((2,)), dma((2,))]
             + [dma((1,)), dma((1,))]
             + [dma((3, 2))],
-            compiler_params=params(38, collective_id=0, has_side_effects=True),
+            compiler_params=params(34, collective_id=0, has_side_effects=True),
             name="summed",
         )(*terms, *weights, *m, *v)
 
-    def settled(arrays, t, own, far, near, m, moment=()):
+    def settled(arrays, t, own, far, near, m, moments=(), crossed=()):
         layers, rows = m[0].shape[0], m[arrays[0]].shape[1]
-        through = ((n - 1) * CORES - 3) * len(arrays) * layers * PARTS
-        jobs = (n - 1) * CORES * len(arrays) * layers * PARTS + (len(pieces_of(layers)) if moment else 0)
+        jobs = (n - 1) * CORES * len(arrays) * layers * PARTS
+        held = 3 * len(arrays) * layers * PARTS + sum(one.shape[0] for one in crossed)
+        through = jobs - held
         size = rows // PARTS * t[0].shape[2]
-        moved_bytes = 2 * size * (jobs + through)
-        results = [like(one) for one in m] if moment else []
+        moved_bytes = 2 * size * (jobs + through) + sum(4 * one.size for pair in moments for one in pair)
+        results = [like(one) for _ in moments for one in m]
         return pl.pallas_call(
-            functools.partial(settle, n, layers, arrays, rows, bool(moment)),
+            functools.partial(settle, n, layers, arrays, rows, len(moments), len(crossed)),
             out_shape=[like(one) for one in t] + results,
-            in_specs=[hbm] * len(t) + [vmem] * (5 + len(moment)),
+            in_specs=[hbm] * len(t) + [vmem] * (5 + 2 * len(moments) + len(crossed)),
             out_specs=[hbm] * (len(t) + len(results)),
-            scratch_shapes=[pltpu.VMEM((through, rows // PARTS, t[0].shape[2]), bf), dma((-(-through // READS) + 4,))],
+            scratch_shapes=[pltpu.VMEM((through, rows // PARTS, t[0].shape[2]), bf), dma((-(-through // READS) + 2 + 2 * len(moments),))],
             compiler_params=params(2 * size * through // 2**20 + 2),
             cost_estimate=pl.CostEstimate(flops=60 * moved_bytes, bytes_accessed=moved_bytes, transcendentals=0),
             name="settle",
-        )(*(pltpu.with_memory_space_constraint(one, pltpu.HBM) for one in t), own, *far, *near, *moment)
-
-    def settled_moment(m, moment):
-        layers = m[0].shape[0]
-        size = 4 * sum(one.size for one in m)
-        return pl.pallas_call(
-            functools.partial(settle_moment, layers),
-            out_shape=[like(one) for one in m],
-            in_specs=[vmem] * 2,
-            out_specs=[hbm] * 3,
-            scratch_shapes=[dma((3,))],
-            compiler_params=params(16),
-            cost_estimate=pl.CostEstimate(flops=60 * size, bytes_accessed=size, transcendentals=0),
-            name="settle_moment",
-        )(*moment)
-
-    def completed(results, came, rows):
+        )(*(pltpu.with_memory_space_constraint(one, pltpu.HBM) for one in t), own, *far, *near, *(one for pair in moments for one in pair), *crossed)
+
+    def completed(arrays, results, came, rows):
         layers = results[0].shape[0]
         return pl.pallas_call(
-            functools.partial(complete, n, layers, rows),
+            functools.partial(complete, n, layers, arrays, rows),
             out_shape=[like(one) for one in results],
-            in_specs=[hbm] * 3 + [vmem] * 8,
-            out_specs=[hbm] * 3,
+            in_specs=[hbm] * len(results) + [vmem] * 4,
+            out_specs=[hbm] * len(results),
             scratch_shapes=[dma((2,))],
-            input_output_aliases={i: i for i in range(3)},
+            input_output_aliases={i: i for i in range(len(results))},
             compiler_params=params(16),
             name="complete",
         )(*results, *came)
@@ -525,15 +524,17 @@
         def cross(came):
             return came + [lax.ppermute(one, "dp", other) for one in came]
 
+        rows = [one.shape[1] for one in m]
         wide = hop(0)
         down = hop(2)
-        new_g, new_u, *ms = settled((0, 1), t[:2], own[0], far[:2], near[:2], m, new_m)
-        (new_d,) = settled((2,), t[2:], own[1], far[2:], near[2:], m)
-        vs = settled_moment(v, new_v)
+        crossed = [lax.ppermute(one, "dp", other) for one in (far[2 + PLUS], near[2 + MINUS])]
+        new_g, new_u, *moments = settled((0, 1), t[:2], own[0], far[:2], near[:2], m, (new_m, new_v))
+        (new_d,) = settled((2,), t[2:], own[1], far[2:], near[2:], m, (), crossed)
         wide = cross(wide)
         down = cross(down)
-        whole = completed((new_g, new_u, new_d), wide + down, [one.shape[1] for one in m])
-        return (*whole, *ms, *vs)
+        new_g, new_u = completed((0, 1), (new_g, new_u), wide, rows[0])
+        (new_d,) = completed((2,), (new_d,), down, rows[2])
+        return (new_g, new_u, new_d, *moments)
 
     all_of, cut = P(None, None, None), P(None, "dp", None)
     return jax.shard_map(

time: 537 us -> 532 us (level)
  transfers between devices with their start and end apart: 8 -> 10, of which waited for: 2 -> 2; matrix products, arithmetic and copies ran while one was open for 0% -> 0% of each run, Pallas kernels for 6% -> 6%
where the time goes in v5:
time: 532 us
  Pallas kernels  493 us (93%)
  waiting for transfers between devices  25.6 us (5%)
  starting transfers between devices  12.6 us (2%)
    pallas_call x1, Pallas kernels, summed(): pl.pallas_call(functools.partial(kernel, n, devices * sum((one.size for o...  458 us
    pallas_call x2, Pallas kernels, settled(): pl.pallas_call(functools.partial(settle, n, layers, arrays, rows, len(mom...  31.3 us
    ppermute x4, waiting for transfers between devices, hop(): lax.ppermute(one, 'dp', way)  25.5 us
  transfers between devices with their start and end apart: 10, of which 2 were waited for; matrix products, arithmetic and copies ran while one was open for 0% of the time, Pallas kernels for 6%

profile of v5, /device:TPU:21, one launch (start us, length us, event | category | flops | bytes accessed | tf_op | source)
XLA Modules:
  0.0 531.8 jit_solution(8955945739337234485)
XLA Ops:
  0.6 458.2 %summed.1 = (bf16[2,512,8192]{2,1,0:T(8,128)(2,1)}, bf16[2,512,8192]{2,1,0:T(8,128)(2,1)}, bf16[2,8192,512]{2,1,0:T(8,128)(2,1)}, bf16[64,16,8192]{2,1,0:T(8,128...) custom-call(bf16[1,2,512,8192]{3,2,1,0:T(8,128)(2,1)} %refs_0_.1, ...), custom_call_target="tpu_custom_call" | custom-call | tf_op jit(solution)/shard_map/summed/pallas_call | solution.py:459
  458.9 0.2 collective-permute-start
  459.1 2.5 collective-permute-start.1
  461.7 1.5 collective-permute-start.4
  463.2 0.0 collective-permute-start.6
  463.2 2.7 collective-permute-start.7
  465.9 18.1 %collective-permute-done.refs_2_ = bf16[4,16,8192]{2,1,0:T(8,128)(2,1)S(1)} collective-permute-done((bf16[4,16,8192]{2,1,0:T(8,128)(2,1)S(1)}, bf16[4,16,8192]{2,1,0:T(8,128)(2,1)S(1)}, u32[]{:S(2)}, u32[]{:S(2)}) %collective-permute-start) | collective-permute-done | bytes 1048608 | tf_op jit(solution)/shard_map/ppermute | solution.py:522
  483.9 3.3 collective-permute-start.2
  487.2 0.0 collective-permute-done.1.refs_3_
  487.2 0.0 collective-permute-start.3
  487.2 0.0 collective-permute-done.4.refs_6_
  487.2 0.5 collective-permute-start.5
  487.7 7.5 %collective-permute-done.6.refs_1_ = bf16[2,256,512]{2,1,0:T(8,128)(2,1)S(1)} collective-permute-done((bf16[2,256,512]{2,1,0:T(8,128)(2,1)S(1)}, bf16[2,256,512]{2,1,0:T(8,128)(2,1)S(1)}, u32[]{:S(2)}, u32[]{:S(2)}) %collective-permute-start.6) | collective-permute-done | bytes 524320 | tf_op jit(solution)/shard_map/ppermute | solution.py:522
  495.2 1.8 collective-permute-start.8
  497.0 0.0 collective-permute-done.7.refs_2_
  497.0 0.0 collective-permute-start.9
  497.0 22.2 %settle.2 = (bf16[2,512,8192]{2,1,0:T(8,128)(2,1)}, bf16[2,512,8192]{2,1,0:T(8,128)(2,1)}, f32[2,32,8192]{2,1,0:T(8,128)}, f32[2,32,8192]{2,1,0:T(8,128)}, f32[2...) custom-call(bf16[2,512,8192]{2,1,0:T(8,128)(2,1)} %get-tuple-element.36.refs_0_, ...), custom_call_target="tpu_custom_call" | custom-call | flops 3900702720 | bytes 65011712 | tf_op jit(solution)/shard_map/settle/pallas_call | solution.py:487
  519.2 0.0 collective-permute-done.5.refs_7_
  519.2 9.1 %settle.3.refs_0_ = bf16[2,8192,512]{2,1,0:T(8,128)(2,1)} custom-call(bf16[2,8192,512]{2,1,0:T(8,128)(2,1)} %get-tuple-element.51.refs_0_, bf16[4,256,512]{2,1,0:T(8,128)(2,1)S(1)} %get-tuple-element.52.refs_1_, bf16[2,256,512]{2,1,0:T(8,128)(2,1)S(1)} %get-tuple-element.53.refs_2_, bf16[2,256,512]{2,1,0:T(8,128)(2,1)S(1)} %get-tuple-element.54.refs_3_, ...), custom_call_target="tpu_custom_call" | custom-call | flops 1509949440 | bytes 25165824 | tf_op jit(solution)/shard_map/settle/pallas_call | solution.py:487
  528.4 0.0 collective-permute-done.8.refs_3_
  528.4 0.0 collective-permute-done.9.refs_4_
  528.4 1.3 complete.3
  529.7 0.0 collective-permute-done.2.refs_4_
  529.8 2.0 complete.2
  (1 shorter events, 0.0 us)
Async XLA Ops:
  458.9 25.1 %collective-permute-start = (bf16[4,16,8192]{2,1,0:T(8,128)(2,1)S(1)}, bf16[4,16,8192]{2,1,0:T(8,128)(2,1)S(1)}, u32[]{:S(2)}, u32[]{:S(2)}) collective-permute-start(bf16[4,16,8192]{2,1,0:T(8,128)(2,1)S(1)} %get-tuple-element.39.refs_3_), channel_id=1, source_target_pairs={{0,2},{1,3},{2,4},{3,5},{4,6},{5,7},{6,8},{7,9},{8,10},{9,11},{10,... | collective-permute-start | bytes 3145736 | tf_op jit(solution)/shard_map/ppermute | solution.py:522
  459.1 28.1 %collective-permute-start.1 = (bf16[4,16,8192]{2,1,0:T(8,128)(2,1)S(1)}, bf16[4,16,8192]{2,1,0:T(8,128)(2,1)S(1)}, u32[]{:S(2)}, u32[]{:S(2)}) collective-permute-start(bf16[4,16,8192]{2,1,0:T(8,128)(2,1)S(1)} %get-tuple-element.40.refs_4_), channel_id=1, source_target_pairs={{2,0},{3,1},{4,2},{5,3},{6,4},{7,5},{8,6},{9,7},{10,8},{11,9},{12,... | collective-permute-start | bytes 3145736 | tf_op jit(solution)/shard_map/ppermute | solution.py:522
  461.7 25.5 %collective-permute-start.4 = (bf16[2,256,512]{2,1,0:T(8,128)(2,1)S(1)}, bf16[2,256,512]{2,1,0:T(8,128)(2,1)S(1)}, u32[]{:S(2)}, u32[]{:S(2)}) collective-permute-start(bf16[2,256,512]{2,1,0:T(8,128)(2,1)S(1)} %get-tuple-element.53.refs_2_), channel_id=1, source_target_pairs={{0,1},{1,0},{2,3},{3,2},{4,5},{5,4},{6,7},{7,6},{8,9},{9,8},{10,11... | collective-permute-start | bytes 1572872 | tf_op jit(solution)/shard_map/ppermute | solution.py:530
  463.2 32.0 %collective-permute-start.6 = (bf16[2,256,512]{2,1,0:T(8,128)(2,1)S(1)}, bf16[2,256,512]{2,1,0:T(8,128)(2,1)S(1)}, u32[]{:S(2)}, u32[]{:S(2)}) collective-permute-start(bf16[2,256,512]{2,1,0:T(8,128)(2,1)S(1)} %get-tuple-element.53.refs_2_), channel_id=1, source_target_pairs={{0,2},{1,3},{2,4},{3,5},{4,6},{5,7},{6,8},{7,9},{8,10},{9,11},{10,... | collective-permute-start | bytes 1572872 | tf_op jit(solution)/shard_map/ppermute | solution.py:522
  463.2 33.8 %collective-permute-start.7 = (bf16[2,256,512]{2,1,0:T(8,128)(2,1)S(1)}, bf16[2,256,512]{2,1,0:T(8,128)(2,1)S(1)}, u32[]{:S(2)}, u32[]{:S(2)}) collective-permute-start(bf16[2,256,512]{2,1,0:T(8,128)(2,1)S(1)} %get-tuple-element.54.refs_3_), channel_id=1, source_target_pairs={{2,0},{3,1},{4,2},{5,3},{6,4},{7,5},{8,6},{9,7},{10,8},{11,9},{12,... | collective-permute-start | bytes 1572872 | tf_op jit(solution)/shard_map/ppermute | solution.py:522
  483.9 45.8 %collective-permute-start.2 = (bf16[4,16,8192]{2,1,0:T(8,128)(2,1)S(1)}, bf16[4,16,8192]{2,1,0:T(8,128)(2,1)S(1)}, u32[]{:S(2)}, u32[]{:S(2)}) collective-permute-start(bf16[4,16,8192]{2,1,0:T(8,128)(2,1)S(1)} %collective-permute-done.refs_2_), channel_id=1, source_target_pairs={{0,1},{1,0},{2,3},{3,2},{4,5},{5,4},{6,7},{7,6},{8,9},{9,8},{10,11... | collective-permute-start | bytes 3145736 | tf_op jit(solution)/shard_map/ppermute | solution.py:525
  487.2 42.6 %collective-permute-start.3 = (bf16[4,16,8192]{2,1,0:T(8,128)(2,1)S(1)}, bf16[4,16,8192]{2,1,0:T(8,128)(2,1)S(1)}, u32[]{:S(2)}, u32[]{:S(2)}) collective-permute-start(bf16[4,16,8192]{2,1,0:T(8,128)(2,1)S(1)} %collective-permute-done.1.refs_3_), channel_id=1, source_target_pairs={{0,1},{1,0},{2,3},{3,2},{4,5},{5,4},{6,7},{7,6},{8,9},{9,8},{10,11... | collective-permute-start | bytes 3145736 | tf_op jit(solution)/shard_map/ppermute | solution.py:525
  487.2 32.0 %collective-permute-start.5 = (bf16[2,256,512]{2,1,0:T(8,128)(2,1)S(1)}, bf16[2,256,512]{2,1,0:T(8,128)(2,1)S(1)}, u32[]{:S(2)}, u32[]{:S(2)}) collective-permute-start(bf16[2,256,512]{2,1,0:T(8,128)(2,1)S(1)} %get-tuple-element.56.refs_5_), channel_id=1, source_target_pairs={{0,1},{1,0},{2,3},{3,2},{4,5},{5,4},{6,7},{7,6},{8,9},{9,8},{10,11... | collective-permute-start | bytes 1572872 | tf_op jit(solution)/shard_map/ppermute | solution.py:530
  495.2 33.2 %collective-permute-start.8 = (bf16[2,256,512]{2,1,0:T(8,128)(2,1)S(1)}, bf16[2,256,512]{2,1,0:T(8,128)(2,1)S(1)}, u32[]{:S(2)}, u32[]{:S(2)}) collective-permute-start(bf16[2,256,512]{2,1,0:T(8,128)(2,1)S(1)} %collective-permute-done.6.refs_1_), channel_id=1, source_target_pairs={{0,1},{1,0},{2,3},{3,2},{4,5},{5,4},{6,7},{7,6},{8,9},{9,8},{10,11... | collective-permute-start | bytes 1572872 | tf_op jit(solution)/shard_map/ppermute | solution.py:525
  497.0 31.4 %collective-permute-start.9 = (bf16[2,256,512]{2,1,0:T(8,128)(2,1)S(1)}, bf16[2,256,512]{2,1,0:T(8,128)(2,1)S(1)}, u32[]{:S(2)}, u32[]{:S(2)}) collective-permute-start(bf16[2,256,512]{2,1,0:T(8,128)(2,1)S(1)} %collective-permute-done.7.refs_2_), channel_id=1, source_target_pairs={{0,1},{1,0},{2,3},{3,2},{4,5},{5,4},{6,7},{7,6},{8,9},{9,8},{10,11... | collective-permute-start | bytes 1572872 | tf_op jit(solution)/shard_map/ppermute | solution.py:525

commit v6 on v5

--- a/solution.py
+++ b/solution.py
@@ -12,6 +12,7 @@
 CORES = 2
 PLUS, MINUS = WAYS = 0, 1
 PARTS = 2
+LEAD = 2
 DOWN = 2
 
 
@@ -99,8 +100,8 @@
     xs, ms, vs, own_new = (refs[i : i + 2] for i in range(15, 23, 2))
     far = {way: refs[23 + 2 * way : 25 + 2 * way] for way in WAYS}
     near = {way: refs[27 + 2 * way : 29 + 2 * way] for way in WAYS}
-    landed, st_own, st_other, old = (refs[i : i + 2] for i in range(31, 39, 2))
-    squares, rs_send, rs_recv, x_send, x_recv, st_sem, ag_send, ag_recv, y_send, y_recv, sq_send, sq_recv, in_sem = refs[39:]
+    landed, st_own, st_other = (refs[i : i + 2] for i in range(31, 37, 2))
+    squares, lead, rs_send, rs_recv, x_send, x_recv, st_sem, ag_send, ag_recv, y_send, y_recv, sq_send, sq_recv, in_sem, lead_sem = refs[37:]
 
     layers = m[0].shape[0]
     rows = [a.shape[1] for a in m]
@@ -157,7 +158,12 @@
         way, d, q = todo[i]
         kind, k = x_at[i]
         dst = (st_other if early(i) else xs)[kind].at[k]
-        return remote(term(q, at(target(way, d), 1 - c)), dst, x_send.at[kind], x_recv.at[term_groups[0][i]], partner)
+        src = lead.at[i] if i < LEAD else term(q, at(target(way, d), 1 - c))
+        return remote(src, dst, x_send.at[kind], x_recv.at[term_groups[0][i]], partner)
+
+    def lead_in(i):
+        way, d, q = todo[i]
+        return pltpu.make_async_copy(term(q, at(target(way, d), 1 - c)), lead.at[i], lead_sem.at[i])
 
     def stage(i):
         way, d, q = todo[i]
@@ -217,10 +223,18 @@
         return (
             pltpu.make_async_copy(m[q[0]].at[part], kept(ms, q), in_sem.at[0, kind_of(q)]),
             pltpu.make_async_copy(v[q[0]].at[part], kept(vs, q), in_sem.at[1, kind_of(q)]),
-            pltpu.make_async_copy(block(w, q, me), kept(old, q), in_sem.at[2, kind_of(q)]),
         )
 
+    def old(q):
+        kind, k = place(q, pieces)
+        return st_own[kind].at[k] if k < depth[kind] else st_other[kind].at[k - depth[kind]]
+
+    def load_weight(q):
+        return pltpu.make_async_copy(block(w, q, me), old(q), in_sem.at[2, kind_of(q)])
+
     window, reach = 24, 3
+    for i in range(LEAD):
+        lead_in(i).start()
     first = [i for i in range(len(todo)) if early(i)]
     for i in first:
         stage_start(i)
@@ -229,6 +243,8 @@
         pl.semaphore_signal(barrier, inc=1, device_id={"dp": to}, device_id_type=MESH)
     pl.semaphore_wait(barrier, 3)
     for i in range(window):
+        if i < LEAD:
+            lead_in(i).wait()
         exchange(i).start()
     total = jnp.zeros((8, 128), jnp.float32)
     for i, s in enumerate(todo):
@@ -272,17 +288,19 @@
 
     for j in sorted(range(1, devices), key=lambda j: -min(j, devices - j)):
         share(j).start()
+    for q in pieces:
+        load_weight(q).start()
     for kind in (0, 1):
         waited(xs[kind], x_send.at[kind])
         waited(several(sum(kind_of(s[2]) == kind for s in items), landed[kind]), rs_send.at[kind])
-        for which, pair in enumerate((ms, vs, old)):
+        for which, pair in enumerate((ms, vs, own_new)):
             waited(pair[kind], in_sem.at[which, kind])
     waited(several(devices - 1, squares), sq_recv.at[0])
     everyone = jnp.sum(jnp.sum(squares[...], axis=0), axis=(0, 1), keepdims=True)
     factor = jnp.minimum(1.0, 0.5 * lax.rsqrt(jnp.broadcast_to(everyone, (8, 128)) / count_all + 1e-30))[0:1, 0:1]
 
-    def stepped(q):
-        wn, mr, vr, wr = kept(own_new, q), kept(ms, q), kept(vs, q), kept(old, q)
+    def stepped(q, share_of=(0, 1)):
+        wn, mr, vr, wr = kept(own_new, q), kept(ms, q), kept(vs, q), old(q)
         cuts, cut = slices(kind_of(q), wn.shape, 8192)
 
         def one(j, _):
@@ -296,7 +314,7 @@
             wn[part] = (before - 0.02 * (mm * lax.rsqrt(vv + 1e-8) + 0.1 * before)).astype(wn.dtype)
             return None
 
-        lax.fori_loop(0, cuts, one, None)
+        lax.fori_loop(cuts * share_of[0] // share_of[1], cuts * (share_of[0] + 1) // share_of[1], one, None)
 
     gathers = [(way, h, q) for h in range(1, half) for q in pieces for way in WAYS]
 
@@ -307,20 +325,29 @@
         kind, k = place(q, among)
         return which[way][kind].at[k]
 
-    def pass_on(s):
+    def pass_on(s, columns=None):
         way, h, q = s
         owner = at(z - step[way] * (h - 1), c)
         group = way * len(gather_groups[1]) + gather_groups[0][gathers.index(s) // 2]
-        src = kept(own_new, q) if h == 1 else block(t, q, owner)
-        return remote(src, lies(way, h, q, owner), ag_send.at[kind_of(q)], ag_recv.at[group], ahead[way])
+        src = kept(own_new, q) if h == 1 else lies(way, h - 1, q, owner)
+        dst = lies(way, h, q, owner)
+        if columns is not None:
+            src, dst = src.at[:, columns], dst.at[:, columns]
+        return remote(src, dst, ag_send.at[kind_of(q)], ag_recv.at[group], ahead[way])
 
     def across(q, owner, src):
         return remote(src, block(t, q, owner), y_send.at[kind_of(q)], y_recv.at[kind_of(q)], partner)
 
     for q in pieces:
-        stepped(q)
-        for way in WAYS:
-            pass_on((way, 1, q)).start()
+        quarter = t[0].shape[2] // 4
+        for k in range(4 if q == pieces[0] else 0):
+            stepped(q, (k, 4))
+            for way in WAYS:
+                pass_on((way, 1, q), pl.ds(k * quarter, quarter)).start()
+        if q != pieces[0]:
+            stepped(q)
+            for way in WAYS:
+                pass_on((way, 1, q)).start()
         across(q, me, kept(own_new, q)).start()
     for i, s in enumerate(gathers):
         way, h, q = s
@@ -376,11 +403,11 @@
     return sets
 
 
-def settle(n, layers, arrays, rows, moments, lates, *refs):
+def settle(n, layers, arrays, rows, moments, *refs):
     refs = list(refs)
     take = lambda number: [refs.pop(0) for _ in range(number)]
     t, own, far, near = take(len(arrays)), take(1)[0], take(2), take(2)
-    pairs, crossed = [take(2) for _ in range(moments)], take(lates)
+    pairs = [take(2) for _ in range(moments)]
     outs, results = take(len(arrays)), [take(3) for _ in range(moments)]
     buf, sem = refs
     half = n // 2
@@ -398,16 +425,17 @@
                 if a not in arrays:
                     continue
                 dst = row_part(outs[arrays.index(a)], layer, part, rows, owner)
-                src = None
+                src, left = None, False
                 if core == 0 and off == 0:
                     src = own.at[place(q, pieces)[1]]
-                for way, come in ((PLUS, n - (half - 1)), (MINUS, half - 1)):
-                    if off == come:
+                for way in WAYS:
+                    hops = n - off if way == PLUS else off
+                    if hops == half - 1 and core == 0:
                         which, among = (far, far_half(way, layers)) if q in far_half(way, layers) else (near, half_of(way, layers))
-                        if core == 0:
-                            src = which[way].at[place(q, among)[1]]
-                        elif late(n, way, half - 1, q):
-                            src = crossed[way].at[place(q, among)[1]]
+                        src = which[way].at[place(q, among)[1]]
+                    left = left or (core == 1 and late(n, way, hops, q))
+                if left:
+                    continue
                 if src is not None:
                     held.append((src, dst))
                 else:
@@ -418,9 +446,10 @@
     moved(sem, through, buf, direct)
 
 
-def complete(n, layers, arrays, rows, *refs):
+def complete(n, layers, arrays, rows, lates, *refs):
     k = len(arrays)
-    came, outs, sem = refs[k : k + 4], refs[k + 4 : 2 * k + 4], refs[2 * k + 4]
+    came, crossed = refs[k : k + 4], refs[k + 4 : k + 4 + lates]
+    outs, sem = refs[k + 4 + lates : 2 * k + 4 + lates], refs[2 * k + 4 + lates]
     me = lax.axis_index("dp")
     z, c = me // CORES, me % CORES
     copies = []
@@ -431,6 +460,13 @@
                 if q[0] in arrays:
                     src = came[2 * core + way].at[place(q, far_half(way, layers))[1]]
                     copies.append((src, row_part(outs[arrays.index(q[0])], q[1], q[2], rows, owner)))
+    hops = n // 2 - 1
+    for way, ref in zip(WAYS, crossed):
+        owner = lax.rem(z + (n - hops if way == PLUS else hops), n) * CORES + 1 - c
+        for q in pieces_of(layers):
+            if late(n, way, hops, q):
+                among = far_half(way, layers) if q in far_half(way, layers) else half_of(way, layers)
+                copies.append((ref.at[place(q, among)[1]], row_part(outs[arrays.index(q[0])], q[1], q[2], rows, owner)))
     moved(sem, direct=[(copies, outs[0].at[0, pl.ds(0, len(copies) * (rows // PARTS))])])
 
 
@@ -462,51 +498,51 @@
             in_specs=[hbm] * 12,
             out_specs=[hbm] * len(outs) + [vmem] * len(held),
             scratch_shapes=pair(pltpu.VMEM, count, bf)
-            + 2 * pair(pltpu.VMEM, (4, 2), bf)
-            + pair(pltpu.VMEM, whole, bf)
-            + [pltpu.VMEM((devices, 8, 128), f32)]
+            + 2 * pair(pltpu.VMEM, [-(-number // 2) for number in whole], bf)
+            + [pltpu.VMEM((devices, 8, 128), f32), pltpu.VMEM((LEAD, *shapes[0]), bf)]
             + [dma((2,)), dma((2 * len(ring_groups[1]),))]
             + [dma((2,)), dma((len(term_groups[1]),))]
-            + [dma((2, 6))]
+            + [dma((2, sum(-(-number // 2) for number in whole)))]
             + [dma((2,)), dma((2 * len(gather_groups[1]),))]
             + [dma((2,)), dma((2,))]
             + [dma((1,)), dma((1,))]
-            + [dma((3, 2))],
-            compiler_params=params(34, collective_id=0, has_side_effects=True),
+            + [dma((3, 2)), dma((LEAD,))],
+            compiler_params=params(31, collective_id=0, has_side_effects=True),
             name="summed",
         )(*terms, *weights, *m, *v)
 
-    def settled(arrays, t, own, far, near, m, moments=(), crossed=()):
+    def settled(arrays, t, own, far, near, m, moments=()):
         layers, rows = m[0].shape[0], m[arrays[0]].shape[1]
         jobs = (n - 1) * CORES * len(arrays) * layers * PARTS
-        held = 3 * len(arrays) * layers * PARTS + sum(one.shape[0] for one in crossed)
+        jobs -= sum(late(n, way, n // 2 - 1, q) and q[0] in arrays for way in WAYS for q in pieces_of(layers))
+        held = 3 * len(arrays) * layers * PARTS
         through = jobs - held
         size = rows // PARTS * t[0].shape[2]
         moved_bytes = 2 * size * (jobs + through) + sum(4 * one.size for pair in moments for one in pair)
         results = [like(one) for _ in moments for one in m]
         return pl.pallas_call(
-            functools.partial(settle, n, layers, arrays, rows, len(moments), len(crossed)),
+            functools.partial(settle, n, layers, arrays, rows, len(moments)),
             out_shape=[like(one) for one in t] + results,
-            in_specs=[hbm] * len(t) + [vmem] * (5 + 2 * len(moments) + len(crossed)),
+            in_specs=[hbm] * len(t) + [vmem] * (5 + 2 * len(moments)),
             out_specs=[hbm] * (len(t) + len(results)),
             scratch_shapes=[pltpu.VMEM((through, rows // PARTS, t[0].shape[2]), bf), dma((-(-through // READS) + 2 + 2 * len(moments),))],
-            compiler_params=params(2 * size * through // 2**20 + 2),
+            compiler_params=params(-(-2 * size * through // 2**20) + 1),
             cost_estimate=pl.CostEstimate(flops=60 * moved_bytes, bytes_accessed=moved_bytes, transcendentals=0),
             name="settle",
-        )(*(pltpu.with_memory_space_constraint(one, pltpu.HBM) for one in t), own, *far, *near, *(one for pair in moments for one in pair), *crossed)
-
-    def completed(arrays, results, came, rows):
+        )(*(pltpu.with_memory_space_constraint(one, pltpu.HBM) for one in t), own, *far, *near, *(one for pair in moments for one in pair))
+
+    def completed(arrays, results, came, rows, crossed=()):
         layers = results[0].shape[0]
         return pl.pallas_call(
-            functools.partial(complete, n, layers, arrays, rows),
+            functools.partial(complete, n, layers, arrays, rows, len(crossed)),
             out_shape=[like(one) for one in results],
-            in_specs=[hbm] * len(results) + [vmem] * 4,
+            in_specs=[hbm] * len(results) + [vmem] * (4 + len(crossed)),
             out_specs=[hbm] * len(results),
             scratch_shapes=[dma((2,))],
             input_output_aliases={i: i for i in range(len(results))},
-            compiler_params=params(16),
+            compiler_params=params(8),
             name="complete",
-        )(*results, *came)
+        )(*results, *came, *crossed)
 
     def step(*arrays):
         terms, weights, m, v = (arrays[i : i + 3] for i in (0, 3, 6, 9))
@@ -529,11 +565,11 @@
         down = hop(2)
         crossed = [lax.ppermute(one, "dp", other) for one in (far[2 + PLUS], near[2 + MINUS])]
         new_g, new_u, *moments = settled((0, 1), t[:2], own[0], far[:2], near[:2], m, (new_m, new_v))
-        (new_d,) = settled((2,), t[2:], own[1], far[2:], near[2:], m, (), crossed)
+        (new_d,) = settled((2,), t[2:], own[1], far[2:], near[2:], m)
         wide = cross(wide)
         down = cross(down)
         new_g, new_u = completed((0, 1), (new_g, new_u), wide, rows[0])
-        (new_d,) = completed((2,), (new_d,), down, rows[2])
+        (new_d,) = completed((2,), (new_d,), down, rows[2], crossed)
         return (new_g, new_u, new_d, *moments)
 
     all_of, cut = P(None, None, None), P(None, "dp", None)

time: 532 us -> 533 us (level)
  no operation moved by 1% of the time
where the time goes in v6:
time: 533 us; the launch traced here: 532 us
  Pallas kernels  493 us (92%)
  waiting for transfers between devices  25.5 us (5%)
  starting transfers between devices  13.1 us (2%)
    pallas_call x1, Pallas kernels, summed(): pl.pallas_call(functools.partial(kernel, n, devices * sum((one.size for o...  458 us
    pallas_call x2, Pallas kernels, settled(): pl.pallas_call(functools.partial(settle, n, layers, arrays, rows, len(mom...  31.2 us
    ppermute x4, waiting for transfers between devices, hop(): lax.ppermute(one, 'dp', way)  25.5 us
  transfers between devices with their start and end apart: 10, of which 2 were waited for; matrix products, arithmetic and copies ran while one was open for 0% of the time, Pallas kernels for 6%

profile of v6, /device:TPU:21, one launch (start us, length us, event | category | flops | bytes accessed | tf_op | source)
XLA Modules:
  0.0 532.4 jit_solution(3270074574369649556)
XLA Ops:
  0.6 458.1 %summed.1 = (bf16[2,512,8192]{2,1,0:T(8,128)(2,1)}, bf16[2,512,8192]{2,1,0:T(8,128)(2,1)}, bf16[2,8192,512]{2,1,0:T(8,128)(2,1)}, bf16[64,16,8192]{2,1,0:T(8,128...) custom-call(bf16[1,2,512,8192]{3,2,1,0:T(8,128)(2,1)} %refs_0_.1, ...), custom_call_target="tpu_custom_call" | custom-call | tf_op jit(solution)/shard_map/summed/pallas_call | solution.py:495
  458.7 0.1 collective-permute-start
  458.9 2.6 collective-permute-start.1
  461.5 0.0 collective-permute-start.4
  461.5 2.7 collective-permute-start.5
  464.2 2.1 collective-permute-start.8
  466.3 17.5 %collective-permute-done.refs_2_ = bf16[4,16,8192]{2,1,0:T(8,128)(2,1)S(1)} collective-permute-done((bf16[4,16,8192]{2,1,0:T(8,128)(2,1)S(1)}, bf16[4,16,8192]{2,1,0:T(8,128)(2,1)S(1)}, u32[]{:S(2)}, u32[]{:S(2)}) %collective-permute-start) | collective-permute-done | bytes 1048608 | tf_op jit(solution)/shard_map/ppermute | solution.py:558
  483.8 3.3 collective-permute-start.2
  487.0 0.0 collective-permute-done.1.refs_3_
  487.0 0.0 collective-permute-start.3
  487.1 8.0 %collective-permute-done.4.refs_1_ = bf16[2,256,512]{2,1,0:T(8,128)(2,1)S(1)} collective-permute-done((bf16[2,256,512]{2,1,0:T(8,128)(2,1)S(1)}, bf16[2,256,512]{2,1,0:T(8,128)(2,1)S(1)}, u32[]{:S(2)}, u32[]{:S(2)}) %collective-permute-start.4) | collective-permute-done | bytes 524320 | tf_op jit(solution)/shard_map/ppermute | solution.py:558
  495.0 1.8 collective-permute-start.9
  496.9 0.0 collective-permute-done.5.refs_2_
  496.9 0.0 collective-permute-start.6
  496.9 0.0 collective-permute-done.8.refs_5_
  496.9 0.5 collective-permute-start.7
  497.4 9.0 %settle.3.refs_0_ = bf16[2,8192,512]{2,1,0:T(8,128)(2,1)} custom-call(bf16[2,8192,512]{2,1,0:T(8,128)(2,1)} %get-tuple-element.51.refs_0_, bf16[4,256,512]{2,1,0:T(8,128)(2,1)S(1)} %get-tuple-element.52.refs_1_, bf16[2,256,512]{2,1,0:T(8,128)(2,1)S(1)} %get-tuple-element.53.refs_2_, bf16[2,256,512]{2,1,0:T(8,128)(2,1)S(1)} %get-tuple-element.54.refs_3_, ...), custom_call_target="tpu_custom_call" | custom-call | flops 1447034880 | bytes 24117248 | tf_op jit(solution)/shard_map/settle/pallas_call | solution.py:523
  506.4 22.2 %settle.2 = (bf16[2,512,8192]{2,1,0:T(8,128)(2,1)}, bf16[2,512,8192]{2,1,0:T(8,128)(2,1)}, f32[2,32,8192]{2,1,0:T(8,128)}, f32[2,32,8192]{2,1,0:T(8,128)}, f32[2...) custom-call(bf16[2,512,8192]{2,1,0:T(8,128)(2,1)} %get-tuple-element.36.refs_0_, ...), custom_call_target="tpu_custom_call" | custom-call | flops 3900702720 | bytes 65011712 | tf_op jit(solution)/shard_map/settle/pallas_call | solution.py:523
  528.6 0.0 collective-permute-done.9.refs_6_
  528.6 0.0 collective-permute-done.7.refs_4_
  528.6 1.7 complete.3
  530.3 0.0 collective-permute-done.2.refs_4_
  530.3 0.0 collective-permute-done.3.refs_5_
  530.4 2.0 complete.2
  (1 shorter events, 0.0 us)
Async XLA Ops:
  458.7 25.1 %collective-permute-start = (bf16[4,16,8192]{2,1,0:T(8,128)(2,1)S(1)}, bf16[4,16,8192]{2,1,0:T(8,128)(2,1)S(1)}, u32[]{:S(2)}, u32[]{:S(2)}) collective-permute-start(bf16[4,16,8192]{2,1,0:T(8,128)(2,1)S(1)} %get-tuple-element.39.refs_3_), channel_id=1, source_target_pairs={{0,2},{1,3},{2,4},{3,5},{4,6},{5,7},{6,8},{7,9},{8,10},{9,11},{10,... | collective-permute-start | bytes 3145736 | tf_op jit(solution)/shard_map/ppermute | solution.py:558
  458.9 28.2 %collective-permute-start.1 = (bf16[4,16,8192]{2,1,0:T(8,128)(2,1)S(1)}, bf16[4,16,8192]{2,1,0:T(8,128)(2,1)S(1)}, u32[]{:S(2)}, u32[]{:S(2)}) collective-permute-start(bf16[4,16,8192]{2,1,0:T(8,128)(2,1)S(1)} %get-tuple-element.40.refs_4_), channel_id=1, source_target_pairs={{2,0},{3,1},{4,2},{5,3},{6,4},{7,5},{8,6},{9,7},{10,8},{11,9},{12,... | collective-permute-start | bytes 3145736 | tf_op jit(solution)/shard_map/ppermute | solution.py:558
  461.5 33.5 %collective-permute-start.4 = (bf16[2,256,512]{2,1,0:T(8,128)(2,1)S(1)}, bf16[2,256,512]{2,1,0:T(8,128)(2,1)S(1)}, u32[]{:S(2)}, u32[]{:S(2)}) collective-permute-start(bf16[2,256,512]{2,1,0:T(8,128)(2,1)S(1)} %get-tuple-element.53.refs_2_), channel_id=1, source_target_pairs={{0,2},{1,3},{2,4},{3,5},{4,6},{5,7},{6,8},{7,9},{8,10},{9,11},{10,... | collective-permute-start | bytes 1572872 | tf_op jit(solution)/shard_map/ppermute | solution.py:558
  461.5 35.3 %collective-permute-start.5 = (bf16[2,256,512]{2,1,0:T(8,128)(2,1)S(1)}, bf16[2,256,512]{2,1,0:T(8,128)(2,1)S(1)}, u32[]{:S(2)}, u32[]{:S(2)}) collective-permute-start(bf16[2,256,512]{2,1,0:T(8,128)(2,1)S(1)} %get-tuple-element.54.refs_3_), channel_id=1, source_target_pairs={{2,0},{3,1},{4,2},{5,3},{6,4},{7,5},{8,6},{9,7},{10,8},{11,9},{12,... | collective-permute-start | bytes 1572872 | tf_op jit(solution)/shard_map/ppermute | solution.py:558
  464.2 32.7 %collective-permute-start.8 = (bf16[2,256,512]{2,1,0:T(8,128)(2,1)S(1)}, bf16[2,256,512]{2,1,0:T(8,128)(2,1)S(1)}, u32[]{:S(2)}, u32[]{:S(2)}) collective-permute-start(bf16[2,256,512]{2,1,0:T(8,128)(2,1)S(1)} %get-tuple-element.53.refs_2_), channel_id=1, source_target_pairs={{0,1},{1,0},{2,3},{3,2},{4,5},{5,4},{6,7},{7,6},{8,9},{9,8},{10,11... | collective-permute-start | bytes 1572872 | tf_op jit(solution)/shard_map/ppermute | solution.py:566
  483.8 46.5 %collective-permute-start.2 = (bf16[4,16,8192]{2,1,0:T(8,128)(2,1)S(1)}, bf16[4,16,8192]{2,1,0:T(8,128)(2,1)S(1)}, u32[]{:S(2)}, u32[]{:S(2)}) collective-permute-start(bf16[4,16,8192]{2,1,0:T(8,128)(2,1)S(1)} %collective-permute-done.refs_2_), channel_id=1, source_target_pairs={{0,1},{1,0},{2,3},{3,2},{4,5},{5,4},{6,7},{7,6},{8,9},{9,8},{10,11... | collective-permute-start | bytes 3145736 | tf_op jit(solution)/shard_map/ppermute | solution.py:561
  487.0 43.3 %collective-permute-start.3 = (bf16[4,16,8192]{2,1,0:T(8,128)(2,1)S(1)}, bf16[4,16,8192]{2,1,0:T(8,128)(2,1)S(1)}, u32[]{:S(2)}, u32[]{:S(2)}) collective-permute-start(bf16[4,16,8192]{2,1,0:T(8,128)(2,1)S(1)} %collective-permute-done.1.refs_3_), channel_id=1, source_target_pairs={{0,1},{1,0},{2,3},{3,2},{4,5},{5,4},{6,7},{7,6},{8,9},{9,8},{10,11... | collective-permute-start | bytes 3145736 | tf_op jit(solution)/shard_map/ppermute | solution.py:561
  495.0 33.6 %collective-permute-start.9 = (bf16[2,256,512]{2,1,0:T(8,128)(2,1)S(1)}, bf16[2,256,512]{2,1,0:T(8,128)(2,1)S(1)}, u32[]{:S(2)}, u32[]{:S(2)}) collective-permute-start(bf16[2,256,512]{2,1,0:T(8,128)(2,1)S(1)} %get-tuple-element.56.refs_5_), channel_id=1, source_target_pairs={{0,1},{1,0},{2,3},{3,2},{4,5},{5,4},{6,7},{7,6},{8,9},{9,8},{10,11... | collective-permute-start | bytes 1572872 | tf_op jit(solution)/shard_map/ppermute | solution.py:566
  496.9 31.8 %collective-permute-start.6 = (bf16[2,256,512]{2,1,0:T(8,128)(2,1)S(1)}, bf16[2,256,512]{2,1,0:T(8,128)(2,1)S(1)}, u32[]{:S(2)}, u32[]{:S(2)}) collective-permute-start(bf16[2,256,512]{2,1,0:T(8,128)(2,1)S(1)} %collective-permute-done.4.refs_1_), channel_id=1, source_target_pairs={{0,1},{1,0},{2,3},{3,2},{4,5},{5,4},{6,7},{7,6},{8,9},{9,8},{10,11... | collective-permute-start | bytes 1572872 | tf_op jit(solution)/shard_map/ppermute | solution.py:561
  496.9 31.8 %collective-permute-start.7 = (bf16[2,256,512]{2,1,0:T(8,128)(2,1)S(1)}, bf16[2,256,512]{2,1,0:T(8,128)(2,1)S(1)}, u32[]{:S(2)}, u32[]{:S(2)}) collective-permute-start(bf16[2,256,512]{2,1,0:T(8,128)(2,1)S(1)} %collective-permute-done.5.refs_2_), channel_id=1, source_target_pairs={{0,1},{1,0},{2,3},{3,2},{4,5},{5,4},{6,7},{7,6},{8,9},{9,8},{10,11... | collective-permute-start | bytes 1572872 | tf_op jit(solution)/shard_map/ppermute | solution.py:561

commit v7 on v6

--- a/solution.py
+++ b/solution.py
@@ -100,8 +100,9 @@
     xs, ms, vs, own_new = (refs[i : i + 2] for i in range(15, 23, 2))
     far = {way: refs[23 + 2 * way : 25 + 2 * way] for way in WAYS}
     near = {way: refs[27 + 2 * way : 29 + 2 * way] for way in WAYS}
-    landed, st_own, st_other = (refs[i : i + 2] for i in range(31, 37, 2))
-    squares, lead, rs_send, rs_recv, x_send, x_recv, st_sem, ag_send, ag_recv, y_send, y_recv, sq_send, sq_recv, in_sem, lead_sem = refs[37:]
+    middle = refs[31:33]
+    landed, st_own, st_other = (refs[i : i + 2] for i in range(33, 39, 2))
+    squares, lead, rs_send, rs_recv, x_send, x_recv, st_sem, ag_send, ag_recv, y_send, y_recv, sq_send, sq_recv, in_sem, lead_sem = refs[39:]
 
     layers = m[0].shape[0]
     rows = [a.shape[1] for a in m]
@@ -319,6 +320,8 @@
     gathers = [(way, h, q) for h in range(1, half) for q in pieces for way in WAYS]
 
     def lies(way, h, q, owner):
+        if h == half - 2 and q[0] != DOWN:
+            return middle[way].at[place(q, pieces)[1]]
         if h < half - 1:
             return block(t, q, owner)
         which, among = (far, far_half(way, layers)) if q in far_half(way, layers) else (near, half_of(way, layers))
@@ -403,10 +406,10 @@
     return sets
 
 
-def settle(n, layers, arrays, rows, moments, *refs):
+def settle(n, layers, arrays, rows, moments, middles, *refs):
     refs = list(refs)
     take = lambda number: [refs.pop(0) for _ in range(number)]
-    t, own, far, near = take(len(arrays)), take(1)[0], take(2), take(2)
+    t, own, far, near, middle = take(len(arrays)), take(1)[0], take(2), take(2), take(middles)
     pairs = [take(2) for _ in range(moments)]
     outs, results = take(len(arrays)), [take(3) for _ in range(moments)]
     buf, sem = refs
@@ -433,6 +436,8 @@
                     if hops == half - 1 and core == 0:
                         which, among = (far, far_half(way, layers)) if q in far_half(way, layers) else (near, half_of(way, layers))
                         src = which[way].at[place(q, among)[1]]
+                    if hops == half - 2 and core == 0 and middle:
+                        src = middle[way].at[place(q, pieces)[1]]
                     left = left or (core == 1 and late(n, way, hops, q))
                 if left:
                     continue
@@ -444,6 +449,10 @@
     for pair, one in zip(pairs, results, strict=True):
         direct += moment_copies(pair, one, layers)
     moved(sem, through, buf, direct)
+
+
+def settle_moment(layers, *refs):
+    moved(refs[5], direct=moment_copies(refs[:2], refs[2:5], layers))
 
 
 def complete(n, layers, arrays, rows, lates, *refs):
@@ -491,7 +500,7 @@
         whole, part = counts(pieces), counts(half_of(PLUS, layers))
         ring_groups, term_groups, gather_groups = groups_of(n, layers)
         outs = [like(w) for w in weights] + pair(jax.ShapeDtypeStruct, counts([s[2] for s in todo]), bf)
-        held = 2 * pair(pltpu.VMEM, whole, f32) + pair(pltpu.VMEM, whole, bf) + 4 * pair(pltpu.VMEM, part, bf)
+        held = 2 * pair(pltpu.VMEM, whole, f32) + pair(pltpu.VMEM, whole, bf) + 4 * pair(pltpu.VMEM, part, bf) + [pltpu.VMEM((whole[0], *shapes[0]), bf)] * 2
         return pl.pallas_call(
             functools.partial(kernel, n, devices * sum(one.size for one in m)),
             out_shape=outs + held,
@@ -511,25 +520,38 @@
             name="summed",
         )(*terms, *weights, *m, *v)
 
-    def settled(arrays, t, own, far, near, m, moments=()):
+    def settled(arrays, t, own, far, near, middle, m, moments=()):
         layers, rows = m[0].shape[0], m[arrays[0]].shape[1]
         jobs = (n - 1) * CORES * len(arrays) * layers * PARTS
         jobs -= sum(late(n, way, n // 2 - 1, q) and q[0] in arrays for way in WAYS for q in pieces_of(layers))
-        held = 3 * len(arrays) * layers * PARTS
+        held = (3 + len(middle)) * len(arrays) * layers * PARTS
         through = jobs - held
         size = rows // PARTS * t[0].shape[2]
         moved_bytes = 2 * size * (jobs + through) + sum(4 * one.size for pair in moments for one in pair)
         results = [like(one) for _ in moments for one in m]
         return pl.pallas_call(
-            functools.partial(settle, n, layers, arrays, rows, len(moments)),
+            functools.partial(settle, n, layers, arrays, rows, len(moments), len(middle)),
             out_shape=[like(one) for one in t] + results,
-            in_specs=[hbm] * len(t) + [vmem] * (5 + 2 * len(moments)),
+            in_specs=[hbm] * len(t) + [vmem] * (5 + len(middle) + 2 * len(moments)),
             out_specs=[hbm] * (len(t) + len(results)),
             scratch_shapes=[pltpu.VMEM((through, rows // PARTS, t[0].shape[2]), bf), dma((-(-through // READS) + 2 + 2 * len(moments),))],
             compiler_params=params(-(-2 * size * through // 2**20) + 1),
             cost_estimate=pl.CostEstimate(flops=60 * moved_bytes, bytes_accessed=moved_bytes, transcendentals=0),
             name="settle",
-        )(*(pltpu.with_memory_space_constraint(one, pltpu.HBM) for one in t), own, *far, *near, *(one for pair in moments for one in pair))
+        )(*(pltpu.with_memory_space_constraint(one, pltpu.HBM) for one in t), own, *far, *near, *middle, *(one for pair in moments for one in pair))
+
+    def settled_moment(m, moment):
+        size = 4 * sum(one.size for one in m)
+        return pl.pallas_call(
+            functools.partial(settle_moment, m[0].shape[0]),
+            out_shape=[like(one) for one in m],
+            in_specs=[vmem] * 2,
+            out_specs=[hbm] * 3,
+            scratch_shapes=[dma((3,))],
+            compiler_params=params(8),
+            cost_estimate=pl.CostEstimate(flops=60 * size, bytes_accessed=size, transcendentals=0),
+            name="settle_moment",
+        )(*moment)
 
     def completed(arrays, results, came, rows, crossed=()):
         layers = results[0].shape[0]
@@ -550,6 +572,7 @@
         t = out[:3]
         new_m, new_v, own = (out[i : i + 2] for i in (5, 7, 9))
         far, near = (out[11], out[13], out[12], out[14]), (out[15], out[17], out[16], out[18])
+        middle = out[19:21]
         onward = [(i, (i + CORES) % devices) for i in range(devices)]
         back = [(b, a) for a, b in onward]
         other = [(i, i + 1 - 2 * (i % CORES)) for i in range(devices)]
@@ -564,13 +587,14 @@
         wide = hop(0)
         down = hop(2)
         crossed = [lax.ppermute(one, "dp", other) for one in (far[2 + PLUS], near[2 + MINUS])]
-        new_g, new_u, *moments = settled((0, 1), t[:2], own[0], far[:2], near[:2], m, (new_m, new_v))
-        (new_d,) = settled((2,), t[2:], own[1], far[2:], near[2:], m)
+        new_g, new_u, *moments = settled((0, 1), t[:2], own[0], far[:2], near[:2], middle, m, (new_m,))
+        vs = settled_moment(v, new_v)
+        (new_d,) = settled((2,), t[2:], own[1], far[2:], near[2:], (), m)
         wide = cross(wide)
         down = cross(down)
         new_g, new_u = completed((0, 1), (new_g, new_u), wide, rows[0])
         (new_d,) = completed((2,), (new_d,), down, rows[2], crossed)
-        return (new_g, new_u, new_d, *moments)
+        return (new_g, new_u, new_d, *moments, *vs)
 
     all_of, cut = P(None, None, None), P(None, "dp", None)
     return jax.shard_map(

time: 533 us -> 532 us (level)
  no operation moved by 1% of the time
where the time goes in v7:
time: 532 us; the launch traced here: 531 us
  Pallas kernels  492 us (92%)
  waiting for transfers between devices  25.5 us (5%)
  starting transfers between devices  13.1 us (2%)
    pallas_call x1, Pallas kernels, summed(): pl.pallas_call(functools.partial(kernel, n, devices * sum((one.size for o...  458 us
    pallas_call x2, Pallas kernels, settled(): pl.pallas_call(functools.partial(settle, n, layers, arrays, rows, len(mom...  27.6 us
    ppermute x4, waiting for transfers between devices, hop(): lax.ppermute(one, 'dp', way)  25.5 us
  transfers between devices with their start and end apart: 10, of which 2 were waited for; matrix products, arithmetic and copies ran while one was open for 0% of the time, Pallas kernels for 6%

profile of v7, /device:TPU:21, one launch (start us, length us, event | category | flops | bytes accessed | tf_op | source)
XLA Modules:
  0.0 531.5 jit_solution(12963052796861555116)
XLA Ops:
  0.6 458.1 %summed.1 = (bf16[2,512,8192]{2,1,0:T(8,128)(2,1)}, bf16[2,512,8192]{2,1,0:T(8,128)(2,1)}, bf16[2,8192,512]{2,1,0:T(8,128)(2,1)}, bf16[64,16,8192]{2,1,0:T(8,128...) custom-call(bf16[1,2,512,8192]{3,2,1,0:T(8,128)(2,1)} %refs_0_.1, ...), custom_call_target="tpu_custom_call" | custom-call | tf_op jit(solution)/shard_map/summed/pallas_call | solution.py:504
  458.7 0.1 collective-permute-start
  458.9 2.6 collective-permute-start.1
  461.5 0.0 collective-permute-start.4
  461.5 2.7 collective-permute-start.5
  464.2 2.1 collective-permute-start.8
  466.3 17.5 %collective-permute-done.refs_2_ = bf16[4,16,8192]{2,1,0:T(8,128)(2,1)S(1)} collective-permute-done((bf16[4,16,8192]{2,1,0:T(8,128)(2,1)S(1)}, bf16[4,16,8192]{2,1,0:T(8,128)(2,1)S(1)}, u32[]{:S(2)}, u32[]{:S(2)}) %collective-permute-start) | collective-permute-done | bytes 1048608 | tf_op jit(solution)/shard_map/ppermute | solution.py:581
  483.8 3.3 collective-permute-start.2
  487.1 0.0 collective-permute-start.3
  487.1 8.0 %collective-permute-done.4.refs_1_ = bf16[2,256,512]{2,1,0:T(8,128)(2,1)S(1)} collective-permute-done((bf16[2,256,512]{2,1,0:T(8,128)(2,1)S(1)}, bf16[2,256,512]{2,1,0:T(8,128)(2,1)S(1)}, u32[]{:S(2)}, u32[]{:S(2)}) %collective-permute-start.4) | collective-permute-done | bytes 524320 | tf_op jit(solution)/shard_map/ppermute | solution.py:581
  495.0 1.8 collective-permute-start.9
  496.9 0.0 collective-permute-done.5.refs_2_
  496.9 0.0 collective-permute-start.6
  496.9 0.0 collective-permute-done.8.refs_5_
  496.9 0.5 collective-permute-start.7
  497.4 2.7 settle_moment.1
  500.1 9.1 %settle.3.refs_0_ = bf16[2,8192,512]{2,1,0:T(8,128)(2,1)} custom-call(bf16[2,8192,512]{2,1,0:T(8,128)(2,1)} %get-tuple-element.53.refs_0_, bf16[4,256,512]{2,1,0:T(8,128)(2,1)S(1)} %get-tuple-element.54.refs_1_, bf16[2,256,512]{2,1,0:T(8,128)(2,1)S(1)} %get-tuple-element.55.refs_2_, bf16[2,256,512]{2,1,0:T(8,128)(2,1)S(1)} %get-tuple-element.56.refs_3_, ...), custom_call_target="tpu_custom_call" | custom-call | flops 1447034880 | bytes 24117248 | tf_op jit(solution)/shard_map/settle/pallas_call | solution.py:532
  509.1 18.6 %settle.2 = (bf16[2,512,8192]{2,1,0:T(8,128)(2,1)}, bf16[2,512,8192]{2,1,0:T(8,128)(2,1)}, f32[2,32,8192]{2,1,0:T(8,128)}, f32[2,32,8192]{2,1,0:T(8,128)}, f32[2,512,512]{2,1,0:T(8,128)}) custom-call(bf16[2,512,8192]{2,1,0:T(8,128)(2,1)} %get-tuple-element.38.refs_0_, bf16[2,512,8192]{2,1,0:T(8,128)(2,1)} %get-tuple-element.39.refs_1_, ...), custom_call_target="tpu_custom_call" | custom-call | flops 3271557120 | bytes 54525952 | tf_op jit(solution)/shard_map/settle/pallas_call | solution.py:532
  527.7 0.0 collective-permute-done.6.refs_3_
  527.7 0.0 collective-permute-done.7.refs_4_
  527.7 1.7 complete.3
  529.4 0.0 collective-permute-done.2.refs_4_
  529.5 0.0 collective-permute-done.3.refs_5_
  529.5 2.0 complete.2
  (2 shorter events, 0.0 us)
Async XLA Ops:
  458.7 25.1 %collective-permute-start = (bf16[4,16,8192]{2,1,0:T(8,128)(2,1)S(1)}, bf16[4,16,8192]{2,1,0:T(8,128)(2,1)S(1)}, u32[]{:S(2)}, u32[]{:S(2)}) collective-permute-start(bf16[4,16,8192]{2,1,0:T(8,128)(2,1)S(1)} %get-tuple-element.41.refs_3_), channel_id=1, source_target_pairs={{0,2},{1,3},{2,4},{3,5},{4,6},{5,7},{6,8},{7,9},{8,10},{9,11},{10,... | collective-permute-start | bytes 3145736 | tf_op jit(solution)/shard_map/ppermute | solution.py:581
  458.9 28.2 %collective-permute-start.1 = (bf16[4,16,8192]{2,1,0:T(8,128)(2,1)S(1)}, bf16[4,16,8192]{2,1,0:T(8,128)(2,1)S(1)}, u32[]{:S(2)}, u32[]{:S(2)}) collective-permute-start(bf16[4,16,8192]{2,1,0:T(8,128)(2,1)S(1)} %get-tuple-element.42.refs_4_), channel_id=1, source_target_pairs={{2,0},{3,1},{4,2},{5,3},{6,4},{7,5},{8,6},{9,7},{10,8},{11,9},{12,... | collective-permute-start | bytes 3145736 | tf_op jit(solution)/shard_map/ppermute | solution.py:581
  461.5 33.5 %collective-permute-start.4 = (bf16[2,256,512]{2,1,0:T(8,128)(2,1)S(1)}, bf16[2,256,512]{2,1,0:T(8,128)(2,1)S(1)}, u32[]{:S(2)}, u32[]{:S(2)}) collective-permute-start(bf16[2,256,512]{2,1,0:T(8,128)(2,1)S(1)} %get-tuple-element.55.refs_2_), channel_id=1, source_target_pairs={{0,2},{1,3},{2,4},{3,5},{4,6},{5,7},{6,8},{7,9},{8,10},{9,11},{10,... | collective-permute-start | bytes 1572872 | tf_op jit(solution)/shard_map/ppermute | solution.py:581
  461.5 35.3 %collective-permute-start.5 = (bf16[2,256,512]{2,1,0:T(8,128)(2,1)S(1)}, bf16[2,256,512]{2,1,0:T(8,128)(2,1)S(1)}, u32[]{:S(2)}, u32[]{:S(2)}) collective-permute-start(bf16[2,256,512]{2,1,0:T(8,128)(2,1)S(1)} %get-tuple-element.56.refs_3_), channel_id=1, source_target_pairs={{2,0},{3,1},{4,2},{5,3},{6,4},{7,5},{8,6},{9,7},{10,8},{11,9},{12,... | collective-permute-start | bytes 1572872 | tf_op jit(solution)/shard_map/ppermute | solution.py:581
  464.2 32.7 %collective-permute-start.8 = (bf16[2,256,512]{2,1,0:T(8,128)(2,1)S(1)}, bf16[2,256,512]{2,1,0:T(8,128)(2,1)S(1)}, u32[]{:S(2)}, u32[]{:S(2)}) collective-permute-start(bf16[2,256,512]{2,1,0:T(8,128)(2,1)S(1)} %get-tuple-element.55.refs_2_), channel_id=1, source_target_pairs={{0,1},{1,0},{2,3},{3,2},{4,5},{5,4},{6,7},{7,6},{8,9},{9,8},{10,11... | collective-permute-start | bytes 1572872 | tf_op jit(solution)/shard_map/ppermute | solution.py:589
  483.8 45.6 %collective-permute-start.2 = (bf16[4,16,8192]{2,1,0:T(8,128)(2,1)S(1)}, bf16[4,16,8192]{2,1,0:T(8,128)(2,1)S(1)}, u32[]{:S(2)}, u32[]{:S(2)}) collective-permute-start(bf16[4,16,8192]{2,1,0:T(8,128)(2,1)S(1)} %collective-permute-done.refs_2_), channel_id=1, source_target_pairs={{0,1},{1,0},{2,3},{3,2},{4,5},{5,4},{6,7},{7,6},{8,9},{9,8},{10,11... | collective-permute-start | bytes 3145736 | tf_op jit(solution)/shard_map/ppermute | solution.py:584
  487.1 42.4 %collective-permute-start.3 = (bf16[4,16,8192]{2,1,0:T(8,128)(2,1)S(1)}, bf16[4,16,8192]{2,1,0:T(8,128)(2,1)S(1)}, u32[]{:S(2)}, u32[]{:S(2)}) collective-permute-start(bf16[4,16,8192]{2,1,0:T(8,128)(2,1)S(1)} %collective-permute-done.1.refs_3_), channel_id=1, source_target_pairs={{0,1},{1,0},{2,3},{3,2},{4,5},{5,4},{6,7},{7,6},{8,9},{9,8},{10,11... | collective-permute-start | bytes 3145736 | tf_op jit(solution)/shard_map/ppermute | solution.py:584
  495.0 32.7 %collective-permute-start.9 = (bf16[2,256,512]{2,1,0:T(8,128)(2,1)S(1)}, bf16[2,256,512]{2,1,0:T(8,128)(2,1)S(1)}, u32[]{:S(2)}, u32[]{:S(2)}) collective-permute-start(bf16[2,256,512]{2,1,0:T(8,128)(2,1)S(1)} %get-tuple-element.58.refs_5_), channel_id=1, source_target_pairs={{0,1},{1,0},{2,3},{3,2},{4,5},{5,4},{6,7},{7,6},{8,9},{9,8},{10,11... | collective-permute-start | bytes 1572872 | tf_op jit(solution)/shard_map/ppermute | solution.py:589
  496.9 30.9 %collective-permute-start.6 = (bf16[2,256,512]{2,1,0:T(8,128)(2,1)S(1)}, bf16[2,256,512]{2,1,0:T(8,128)(2,1)S(1)}, u32[]{:S(2)}, u32[]{:S(2)}) collective-permute-start(bf16[2,256,512]{2,1,0:T(8,128)(2,1)S(1)} %collective-permute-done.4.refs_1_), channel_id=1, source_target_pairs={{0,1},{1,0},{2,3},{3,2},{4,5},{5,4},{6,7},{7,6},{8,9},{9,8},{10,11... | collective-permute-start | bytes 1572872 | tf_op jit(solution)/shard_map/ppermute | solution.py:584
  496.9 30.9 %collective-permute-start.7 = (bf16[2,256,512]{2,1,0:T(8,128)(2,1)S(1)}, bf16[2,256,512]{2,1,0:T(8,128)(2,1)S(1)}, u32[]{:S(2)}, u32[]{:S(2)}) collective-permute-start(bf16[2,256,512]{2,1,0:T(8,128)(2,1)S(1)} %collective-permute-done.5.refs_2_), channel_id=1, source_target_pairs={{0,1},{1,0},{2,3},{3,2},{4,5},{5,4},{6,7},{7,6},{8,9},{9,8},{10,11... | collective-permute-start | bytes 1572872 | tf_op jit(solution)/shard_map/ppermute | solution.py:584
